TPU v7x, 32 devices: a 4x4x1 block of a 4x4x8 slice. The times are simulated.
32 devices in a mesh: dp: 1 (over z), tp: 4 (over y), ep: 8 (over x, core).
Axes of the slice: x: 4, y: 4, z: 1, core: 2. Of those that a mesh axis runs over, the one named last changes fastest.
The devices are a block of a 4x4x8 slice.
Arguments:
- tokens: bfloat16 [65536, 768], P(('dp', 'ep'))
- grad_out: bfloat16 [65536, 768], P(('dp', 'ep'))
- w_router: bfloat16 [768, 32], replicated
- w_in: bfloat16 [32, 768, 3072], P('ep', None, 'tp')
- w_out: bfloat16 [32, 3072, 768], P('ep', 'tp')
- expert_ids: int32 [65536], P(('dp', 'ep'))
Outputs:
- output 1: bfloat16 [65536, 768], P(('dp', 'ep'))
- output 2: bfloat16 [65536, 768], P(('dp', 'ep'))
- output 3: float32 [32, 768, 3072], P(('dp', 'ep'), None, 'tp')
- output 4: float32 [32, 3072, 768], P(('dp', 'ep'), 'tp')
- output 5: float32 [768, 32], P('dp')
All inputs are finite; a program needn't handle non-finite values.
Results may differ from a plain program's by a relative error of at most 0.00680241.
Values are sent between devices in bfloat16 or wider.
A program may use at most 768 MiB of HBM per device.

v0:
```python
import jax
import jax.numpy as jnp
from jax import lax
from jax.sharding import PartitionSpec as P


def solution(mesh):
    ep_size = mesh.shape["ep"]
    row_spec = P(("dp", "ep"), None)

    def local_block(tokens, grad_out, w_router, w_in, w_out, expert_ids):
        n_local, d_model = tokens.shape
        n_experts = w_router.shape[1]
        local_experts = w_in.shape[0]
        capacity = (6 * n_local + 5 * n_experts - 1) // (5 * n_experts)
        n_slots = n_experts * capacity
        chosen = expert_ids[:, None] == jnp.arange(n_experts)[None, :]
        one_hot = chosen.astype(jnp.int32)
        position = jnp.sum(jnp.cumsum(one_hot, axis=0) * one_hot, axis=1) - 1
        slot_index = jnp.where(position < capacity, expert_ids * capacity + position, n_slots)

        def dispatch(rows):
            slot_buf = jnp.zeros((n_slots + 1, d_model), rows.dtype).at[slot_index].set(rows)
            send_buf = slot_buf[:n_slots].reshape(ep_size, local_experts, capacity, d_model)
            recv_buf = lax.all_to_all(send_buf, "ep", 0, 2, tiled=True)
            return recv_buf.reshape(local_experts, ep_size * capacity, d_model)

        def combine(expert_rows):
            send_buf = expert_rows.reshape(local_experts, ep_size, capacity, d_model)
            recv_buf = lax.all_to_all(send_buf, "ep", 1, 0, tiled=True)
            padded = jnp.concatenate([recv_buf.reshape(n_slots, d_model), jnp.zeros((1, d_model), expert_rows.dtype)], axis=0)
            return jnp.take(padded, slot_index, axis=0)

        logits = jnp.dot(tokens, w_router, preferred_element_type=jnp.float32)
        router_prob = jax.nn.softmax(logits, axis=-1)
        gate_prob = jnp.sum(jnp.where(chosen, router_prob, 0.0), axis=1)

        slot_rows = dispatch(tokens)
        pre_act = jnp.einsum("erd,edf->erf", slot_rows, w_in, preferred_element_type=jnp.float32)
        act_val, act_vjp = jax.vjp(jax.nn.gelu, pre_act)
        hidden = act_val.astype(jnp.bfloat16)
        y_part = jnp.einsum("erf,efd->erd", hidden, w_out, preferred_element_type=jnp.float32)
        y_rows = lax.psum(y_part, "tp").astype(jnp.bfloat16)
        y_tok = combine(y_rows)
        moe_out = (gate_prob[:, None] * y_tok.astype(jnp.float32)).astype(jnp.bfloat16)

        dy_tok = (gate_prob[:, None] * grad_out.astype(jnp.float32)).astype(jnp.bfloat16)
        dy_rows = dispatch(dy_tok)
        d_hidden = jnp.einsum("erd,efd->erf", dy_rows, w_out, preferred_element_type=jnp.float32)
        d_pre = act_vjp(d_hidden)[0].astype(jnp.bfloat16)
        grad_w_out = jnp.einsum("erf,erd->efd", hidden, dy_rows, preferred_element_type=jnp.float32)
        grad_w_in = jnp.einsum("erd,erf->edf", slot_rows, d_pre, preferred_element_type=jnp.float32)
        d_part = jnp.einsum("erf,edf->erd", d_pre, w_in, preferred_element_type=jnp.float32)
        d_slot = lax.psum(d_part, "tp").astype(jnp.bfloat16)
        dx_moe = combine(d_slot)

        d_gate = jnp.sum(grad_out.astype(jnp.float32) * y_tok.astype(jnp.float32), axis=1)
        d_logits = (d_gate[:, None] * router_prob * (chosen.astype(jnp.float32) - gate_prob[:, None])).astype(jnp.bfloat16)
        router_grad = jnp.einsum("te,de->td", d_logits, w_router, preferred_element_type=jnp.float32)
        grad_tokens = (dx_moe.astype(jnp.float32) + router_grad).astype(jnp.bfloat16)
        grad_w_router = lax.psum(jnp.einsum("td,te->de", tokens, d_logits, preferred_element_type=jnp.float32), "ep")
        return moe_out, grad_tokens, grad_w_in, grad_w_out, grad_w_router

    in_specs = (row_spec, row_spec, P(None, None), P("ep", None, "tp"), P("ep", "tp", None), P(("dp", "ep")))
    out_specs = (row_spec, row_spec, P(("dp", "ep"), None, "tp"), P(("dp", "ep"), "tp", None), P("dp", None))
    return jax.shard_map(local_block, mesh=mesh, in_specs=in_specs, out_specs=out_specs, check_vma=False)
```

profile of v0, /device:TPU:97, one launch (start us, length us, event | category | flops | bytes accessed | tf_op | source)
XLA Modules:
  0.0 2037.7 jit_solution(18344921330381185219)
XLA Ops:
  8.1 9.5 reduce-window.6
  21.9 45.3 %scatter_custom_fusion = bf16[9857,768]{1,0:T(8,128)(2,1)} fusion(s32[8192]{0:T(1024)S(1)} %get-tuple-element.9, bf16[8192,768]{1,0:T(8,128)(2,1)} %param.8, bf16[]{:T(256)} %constant.6.clone.1), kind=kCustom, calls=%fused_computation.33 | custom fusion | bytes 15140864 | tf_op jit(solution)/shard_map/scatter | solution.py:23
  67.3 13.5 slice.22
  80.7 17.3 reshape.64
  98.0 26.0 %copy.17 = bf16[8,4,308,768]{3,1,2,0:T(4,128)(2,1)} copy(bf16[8,4,308,768]{3,2,1,0:T(8,128)(2,1)} %reshape.64) | data formatting | bytes 30277632 | tf_op jit(solution)/shard_map/reshape | solution.py:24
  142.6 47.9 %scatter_custom_fusion.1 = bf16[9857,768]{1,0:T(8,128)(2,1)} fusion(s32[8192]{0:T(1024)S(1)} %get-tuple-element.9, bf16[8192,768]{1,0:T(8,128)(2,1)} %param.9, f32[8192]{0:T(1024)S(1)} %select_reduce_fusion, bf16[]{:T(256)} %constant.6.clone.1), kind=kCustom, calls=%fused_computation.29 | custom fusion | flops 18874368 | bytes 27756034 | tf_op jit(solution)/shard_map/scatter | solution.py:23
  190.4 13.3 slice.23
  203.7 17.3 reshape.68
  221.1 26.0 %copy.21 = bf16[8,4,308,768]{3,1,2,0:T(4,128)(2,1)} copy(bf16[8,4,308,768]{3,2,1,0:T(8,128)(2,1)} %reshape.68) | data formatting | bytes 30277632 | tf_op jit(solution)/shard_map/reshape | solution.py:24
  247.0 51.0 %all-to-all-done = bf16[8,4,308,768]{3,1,2,0:T(4,128)(2,1)} async-done(((bf16[8,4,308,768]{3,1,2,0:T(4,128)(2,1)}), bf16[8,4,308,768]{3,1,2,0:T(4,128)(2,1)}, u32[]{:S(2)}, u32[]{:S(2)}) %all-to-all-start) | async-done | bytes 15138848 | tf_op jit(solution)/shard_map/all_to_all | solution.py:25
  305.0 23.0 %fusion.18 = f32[4,2464,768]{2,1,0:T(8,128)} fusion(bf16[4,768,768]{2,1,0:T(8,128)(2,1)} %param.11, bf16[4,2464,768]{2,0,1:T(4,128)(2,1)} %bitcast.4), kind=kOutput, calls=%fused_computation.27 | convolution fusion | flops 11626610688 | bytes 50135040 | tf_op jit(solution)/shard_map/erd,edf->erf/dot_general | solution.py:39
  328.0 29.3 %fusion.31 = f32[4,2464,768]{2,1,0:T(8,128)} fusion(bf16[4,768,768]{2,1,0:T(8,128)(2,1)} %param.12, f32[4,2464,768]{2,1,0:T(8,128)} %fusion.18), kind=kOutput, calls=%fused_computation.52 | convolution fusion | flops 11694735360 | bytes 65273856 | tf_op jit(solution)/shard_map/erf,efd->erd/dot_general | solution.py:42
  357.2 113.5 %all-to-all-done.2 = bf16[8,4,308,768]{3,1,2,0:T(4,128)(2,1)} async-done(((bf16[8,4,308,768]{3,1,2,0:T(4,128)(2,1)}), bf16[8,4,308,768]{3,1,2,0:T(4,128)(2,1)}, u32[]{:S(2)}, u32[]{:S(2)}) %all-to-all-start.2) | async-done | bytes 15138848 | tf_op jit(solution)/shard_map/all_to_all | solution.py:25
  470.8 36.8 %fusion.6 = bf16[4,2464,768]{2,1,0:T(8,128)(2,1)} fusion(f32[4,2464,768]{2,1,0:T(8,128)} %fusion.18, bf16[4,768,768]{2,1,0:T(8,128)(2,1)} %param.12, bf16[4,2464,768]{2,0,1:T(4,128)(2,1)} %bitcast.10), kind=kOutput, calls=%fused_computation.15 | convolution fusion | flops 11777998848 | bytes 65273856 | tf_op jit(solution)/shard_map/erd,efd->erf/dot_general | solution.py:49
  507.6 22.0 %fusion.33 = f32[4,2464,768]{2,1,0:T(8,128)} fusion(bf16[4,2464,768]{2,1,0:T(8,128)(2,1)} %fusion.6, bf16[4,768,768]{2,1,0:T(8,128)(2,1)} %param.11), kind=kOutput, calls=%fused_computation.54 | convolution fusion | flops 11626610688 | bytes 50135040 | tf_op jit(solution)/shard_map/erf,edf->erd/dot_general | solution.py:53
  529.6 1013.0 %all-reduce.7 = (bf16[4,2464,768]{2,1,0:T(8,128)(2,1)}, bf16[4,2464,768]{2,1,0:T(8,128)(2,1)}) all-reduce(f32[4,2464,768]{2,1,0:T(8,128)} %fusion.31, f32[4,2464,768]{2,1,0:T(8,128)} %fusion.33), channel_id=1, replica_groups=mesh['dp'=1,'tp'=4,'ep'=8] {'tp'}, use_global_device_ids=true, to_apply=%region_7.8 | all-reduce | flops 15138816 | bytes 90832896 | tf_op jit(solution)/shard_map/psum | solution.py:43
  1542.6 39.6 %copy.26 = bf16[4,2464,768]{2,0,1:T(4,128)(2,1)} copy(bf16[4,2464,768]{2,1,0:T(8,128)(2,1)} %get-tuple-element.6) | data formatting | bytes 30277632 | tf_op jit(solution)/shard_map/reshape | solution.py:29
  1582.2 10.0 all-to-all-start.1
  1592.8 39.6 %copy.28 = bf16[4,2464,768]{2,0,1:T(4,128)(2,1)} copy(bf16[4,2464,768]{2,1,0:T(8,128)(2,1)} %get-tuple-element.7) | data formatting | bytes 30277632 | tf_op jit(solution)/shard_map/reshape | solution.py:29
  1632.4 125.7 %all-to-all-done.1 = bf16[4,8,308,768]{3,0,2,1:T(4,128)(2,1)} async-done(((bf16[4,8,308,768]{3,0,2,1:T(4,128)(2,1)}), bf16[4,8,308,768]{3,0,2,1:T(4,128)(2,1)}, u32[]{:S(2)}, u32[]{:S(2)}) %all-to-all-start.1) | async-done | bytes 15138848 | tf_op jit(solution)/shard_map/all_to_all | solution.py:30
  1764.7 21.8 %fusion.16 = f32[4,768,768]{2,1,0:T(8,128)} fusion(bf16[4,2464,768]{2,1,0:T(8,128)(2,1)} %fusion.6, bf16[4,2464,768]{2,0,1:T(4,128)(2,1)} %bitcast.4), kind=kOutput, calls=%fused_computation.25 | convolution fusion | flops 11626610688 | bytes 39714816 | tf_op jit(solution)/shard_map/erd,erf->edf/dot_general | solution.py:52
  1786.5 24.8 %fusion.10 = f32[4,768,768]{2,1,0:T(8,128)} fusion(bf16[4,2464,768]{2,0,1:T(4,128)(2,1)} %bitcast.10, f32[4,2464,768]{2,1,0:T(8,128)} %fusion.18), kind=kOutput, calls=%fused_computation.21 | convolution fusion | flops 11694735360 | bytes 54853632 | tf_op jit(solution)/shard_map/erf,erd->efd/dot_general | solution.py:51
  1811.2 12.0 copy.20
  1823.3 17.3 reshape.67
  1840.6 13.4 concatenate.6
  1854.0 44.3 %gather_fusion = bf16[8192,768]{1,0:T(8,128)(2,1)} fusion(bf16[9857,768]{1,0:T(8,128)(2,1)} %concatenate.6, s32[8192]{0:T(1024)S(1)} %copy-done.11), kind=kCustom, calls=%fused_computation.clone | custom fusion | bytes 25198592 | tf_op jit(solution)/shard_map/jit(_take)/gather | solution.py:32
  1898.4 17.0 fusion.9
  1930.6 12.0 copy.24
  1942.7 17.4 reshape.71
  1960.1 13.4 concatenate.7
  1973.5 44.3 %gather_fusion.1 = bf16[8192,768]{1,0:T(8,128)(2,1)} fusion(bf16[9857,768]{1,0:T(8,128)(2,1)} %concatenate.7, s32[8192]{0:T(1024)S(1)} %copy-done.11), kind=kCustom, calls=%fused_computation.1.clone | custom fusion | bytes 25198592 | tf_op jit(solution)/shard_map/jit(_take)/gather | solution.py:32
  2017.8 11.1 add_convert_fusion
  (49 shorter events, 54.6 us)
Async XLA Ops:
  7.2 125.1 %copy-start = (bf16[768,32]{0,1:T(8,128)(2,1)S(1)}, bf16[768,32]{0,1:T(8,128)(2,1)}, u32[]{:S(2)}) copy-start(bf16[768,32]{0,1:T(8,128)(2,1)} %param.10) | copy-start | bytes 147460
  21.9 120.6 %copy-start.12 = (s32[8192]{0:T(1024)}, s32[8192]{0:T(1024)S(1)}, u32[]{:S(2)}) copy-start(s32[8192]{0:T(1024)S(1)} %get-tuple-element.9) | copy-start | bytes 98308
  124.0 174.0 %all-to-all-start = ((bf16[8,4,308,768]{3,1,2,0:T(4,128)(2,1)}), bf16[8,4,308,768]{3,1,2,0:T(4,128)(2,1)}, u32[]{:S(2)}, u32[]{:S(2)}) async-start(bf16[8,4,308,768]{3,1,2,0:T(4,128)(2,1)} %copy.17), calls=%async_computation | async-start | bytes 30277632 | tf_op jit(solution)/shard_map/all_to_all | solution.py:25
  132.3 10.0 copy-start.3
  140.6 1.0 copy-start.1
  140.6 1.0 copy-start.5
  141.6 0.6 copy-start.9
  142.5 61.2 %copy-start.7 = (f32[8192]{0:T(1024)}, f32[8192]{0:T(1024)S(1)}, u32[]{:S(2)}) copy-start(f32[8192]{0:T(1024)S(1)} %select_reduce_fusion) | copy-start | bytes 98308
  298.0 172.7 %all-to-all-start.2 = ((bf16[8,4,308,768]{3,1,2,0:T(4,128)(2,1)}), bf16[8,4,308,768]{3,1,2,0:T(4,128)(2,1)}, u32[]{:S(2)}, u32[]{:S(2)}) async-start(bf16[8,4,308,768]{3,1,2,0:T(4,128)(2,1)} %copy.21), calls=%async_computation.2 | async-start | bytes 30277632 | tf_op jit(solution)/shard_map/all_to_all | solution.py:25
  1582.2 10.0 copy-start.13
  1582.2 176.0 %all-to-all-start.1 = ((bf16[4,8,308,768]{3,0,2,1:T(4,128)(2,1)}), bf16[4,8,308,768]{3,0,2,1:T(4,128)(2,1)}, u32[]{:S(2)}, u32[]{:S(2)}) async-start(bf16[4,8,308,768]{3,0,2,1:T(4,128)(2,1)} %bitcast.52), calls=%async_computation.1 | async-start | bytes 30277632 | tf_op jit(solution)/shard_map/all_to_all | solution.py:30
  1758.1 172.5 %all-to-all-start.3 = ((bf16[4,8,308,768]{3,0,2,1:T(4,128)(2,1)}), bf16[4,8,308,768]{3,0,2,1:T(4,128)(2,1)}, u32[]{:S(2)}, u32[]{:S(2)}) async-start(bf16[4,8,308,768]{3,0,2,1:T(4,128)(2,1)} %bitcast.51), calls=%async_computation.3 | async-start | bytes 30277632 | tf_op jit(solution)/shard_map/all_to_all | solution.py:30
  1764.7 264.2 %all-reduce.6.cloned.1.call-start = ((), (), s32[]{:S(2)}) async-start(), calls=%async_computation.4 | async-start | bytes 196608 | tf_op jit(solution)/shard_map/psum | solution.py:61
  1840.6 13.4 copy-start.11
  1854.0 44.3 %copy-start.8 = (f32[8192]{0:T(1024)S(1)}, f32[8192]{0:T(1024)}, u32[]{:S(2)}) copy-start(f32[8192]{0:T(1024)} %copy-done.7) | copy-start | bytes 98308
  1854.0 44.3 %copy-start.14 = (pred[8192]{0:T(1024)(128)(4,1)S(1)}, pred[8192]{0:T(1024)(128)(4,1)}, u32[]{:S(2)}) copy-start(pred[8192]{0:T(1024)(128)(4,1)} %get-tuple-element.8) | copy-start | bytes 24580
  1898.3 17.0 copy-start.2
  1898.3 17.0 copy-start.4
  1898.3 17.0 copy-start.6
  1898.4 17.0 copy-start.10
Sparse Core Ops, SparseCore 0:
  1923.0 51.6 all-reduce.5
where the time goes:
time: 2050 us; the launch traced here: 2040 us
  blocking collectives  1010 us (49%)
  local copies, waits for them, and re-layouts  416 us (20%)
  waiting for transfers between devices  298 us (15%)
  matrix products  184 us (9%)
  other arithmetic  79.8 us (4%)
  starting transfers between devices  31.7 us (2%)
    psum x1, blocking collectives, local_block(): y_rows = lax.psum(y_part, 'tp').astype(jnp.bfloat16)  1010 us
    all_to_all x2, waiting for transfers between devices, dispatch(): recv_buf = lax.all_to_all(send_buf, 'ep', 0, 2, tiled=True)  165 us
    all_to_all x2, waiting for transfers between devices, combine(): recv_buf = lax.all_to_all(send_buf, 'ep', 1, 0, tiled=True)  133 us
    gather x2, local copies, waits for them, and re-layouts, combine(): return jnp.take(padded, slot_index, axis=0)  88.6 us
    reshape x4, local copies, waits for them, and re-layouts, dispatch(): slot_buf[:n_slots].reshape(ep_size, local_experts, capacity, d_model)  86.6 us
    reshape x2, local copies, waits for them, and re-layouts, combine(): send_buf = expert_rows.reshape(local_experts, ep_size, capacity, d_model)  79.2 us
    scatter x1, other arithmetic, dispatch(): jnp.zeros((n_slots + 1, d_model), rows.dtype).at[slot_index].set(rows)  47.9 us
    scatter x1, local copies, waits for them, and re-layouts, dispatch(): jnp.zeros((n_slots + 1, d_model), rows.dtype).at[slot_index].set(rows)  45.3 us
  transfers between devices with their start and end apart: 5, of which 4 were waited for; matrix products, arithmetic and copies ran while one was open for 23% of the time, Pallas kernels for 0%

commit v1 on v0

v1 whole, which is shorter than its diff:
```python
import jax
import jax.numpy as jnp
from jax import lax
from jax.sharding import PartitionSpec as P


def solution(mesh):
    ep_size = mesh.shape["ep"]
    tp_size = mesh.shape["tp"]
    row_spec = P(("dp", "ep"), None)
    bf16, f32 = jnp.bfloat16, jnp.float32

    def block(tokens, grad_out, w_router, w_in, w_out, expert_ids):
        n_local, _ = tokens.shape
        n_experts = w_router.shape[1]
        local_experts = w_in.shape[0]
        assert local_experts == tp_size == 4
        capacity = (6 * n_local + 5 * n_experts - 1) // (5 * n_experts)
        cap = (capacity + 7) // 8 * 8
        my_tp = lax.axis_index("tp")

        def from_offset(weight, offset):
            mine = lax.dynamic_index_in_dim(weight, (my_tp - offset) % tp_size, 0, keepdims=False)
            return lax.ppermute(mine, "tp", [(i, (i - offset) % tp_size) for i in range(tp_size)])

        def gather_weight(weight):
            own = lax.dynamic_index_in_dim(weight, my_tp, 0, keepdims=False)
            return jnp.stack([from_offset(weight, 2), own, from_offset(weight, 1), from_offset(weight, 3)])

        wi, wo = gather_weight(w_in), gather_weight(w_out)

        block = 256
        n_blocks = n_local // block
        chosen_t = jnp.arange(n_experts)[:, None] == expert_ids[None, :]
        upper = (jnp.arange(block)[:, None] <= jnp.arange(block)[None, :]).astype(bf16)
        one_hot = chosen_t.astype(bf16).reshape(n_experts * n_blocks, block)
        inside = jnp.dot(one_hot, upper, preferred_element_type=f32).reshape(n_experts, n_blocks, block)
        totals = inside[:, :, -1]
        before = jnp.dot(totals.astype(bf16), (jnp.arange(n_blocks)[:, None] < jnp.arange(n_blocks)[None, :]).astype(bf16), preferred_element_type=f32)
        running = (inside + before[:, :, None]).reshape(n_experts, n_local)
        position = (jnp.sum(jnp.where(chosen_t, running, 0.0), axis=0) - 1.0).astype(jnp.int32)
        kept = position < capacity

        token_ids = jnp.arange(n_local)
        at_slot = (jnp.where(kept, position, cap)[None, :] == jnp.arange(cap)[:, None]).astype(bf16)
        high = (token_ids // 128).astype(f32)
        low = (token_ids % 128).astype(f32)

        def slot_map(row):
            experts = jnp.arange(ep_size) * tp_size + row
            mine = expert_ids[None, :] == experts[:, None]
            digits = jnp.concatenate([jnp.where(mine, high, 0.0), jnp.where(mine, low, 0.0), mine.astype(f32)]).astype(bf16)
            found = lax.dot_general(digits, at_slot, (((1,), (1,)), ((), ())), preferred_element_type=f32).reshape(3, ep_size, cap)
            token = (found[0] * 128.0 + found[1]).astype(jnp.int32)
            filled = found[2] > 0.5
            token = jnp.where(filled, token, token[:, :1])
            return experts, token.reshape(-1), filled.reshape(-1)

        def exchange(rows):
            return lax.all_to_all(rows.reshape(ep_size, cap, rows.shape[1]), "ep", 0, 0, tiled=True).reshape(rows.shape)

        def send_rows(row):
            experts, slot_token, filled = slot_map(row)
            x_send = jnp.take(tokens, slot_token, axis=0, mode="clip")
            gy_send = jnp.take(grad_out, slot_token, axis=0, mode="clip")
            prob = jax.nn.softmax(jnp.dot(x_send, w_router, preferred_element_type=f32), axis=-1)
            slot_expert = jnp.repeat(experts, cap)
            gate = jnp.sum(jnp.where(slot_expert[:, None] == jnp.arange(n_experts)[None, :], prob, 0.0), axis=1)
            gate = jnp.where(filled, gate, 0.0)
            dy_send = (gate[:, None] * gy_send.astype(f32)).astype(bf16)
            return x_send, dy_send

        x_send, dy_send = send_rows(my_tp)
        x_rows = exchange(x_send)
        dy_rows = exchange(dy_send)

        pre_act = jnp.einsum("rd,kdf->krf", x_rows, wi, preferred_element_type=f32)
        act_val, act_vjp = jax.vjp(jax.nn.gelu, pre_act)
        hidden = act_val.astype(bf16)
        y_rows = jnp.einsum("krf,kfd->rd", hidden, wo, preferred_element_type=f32).astype(bf16)
        y_back = exchange(y_rows)
        y_all = lax.all_gather(y_back, "tp", axis=0, tiled=True)

        d_hidden = jnp.einsum("rd,kfd->krf", dy_rows, wo, preferred_element_type=f32)
        d_pre = act_vjp(d_hidden)[0].astype(bf16)
        d_slot = jnp.einsum("krf,kdf->rd", d_pre, wi, preferred_element_type=f32).astype(bf16)
        s_back = exchange(d_slot)
        s_all = lax.all_gather(s_back, "tp", axis=0, tiled=True)

        far_tp = (my_tp + 2) % tp_size
        far_x, far_dy = send_rows(far_tp)
        far_x = exchange(far_x)
        far_dy = exchange(far_dy)
        far_pre = jnp.dot(far_x, lax.dynamic_index_in_dim(w_in, far_tp, 0, keepdims=False), preferred_element_type=f32)
        far_act, far_vjp = jax.vjp(jax.nn.gelu, far_pre)
        far_hidden = far_act.astype(bf16)
        far_dh = lax.dot_general(far_dy, lax.dynamic_index_in_dim(w_out, far_tp, 0, keepdims=False), (((1,), (1,)), ((), ())), preferred_element_type=f32)
        far_dpre = far_vjp(far_dh)[0].astype(bf16)

        def rows_product(left, right):
            return lax.dot_general(left, right, (((0,), (0,)), ((), ())), preferred_element_type=f32)

        def spread(left, right, far_left, far_right):
            own, nxt, prv = [rows_product(left[k] if left.ndim == 3 else left, right[k] if right.ndim == 3 else right) for k in (1, 2, 3)]
            far = rows_product(far_left, far_right)
            up = lax.ppermute(nxt, "tp", [(i, (i + 1) % tp_size) for i in range(tp_size)])
            down = lax.ppermute(prv, "tp", [(i, (i - 1) % tp_size) for i in range(tp_size)])
            grads = jnp.zeros((local_experts,) + own.shape, f32)
            for part, offset in ((own, 0), (far, 2), (up, 3), (down, 1)):
                grads = lax.dynamic_update_index_in_dim(grads, part, (my_tp + offset) % tp_size, 0)
            return grads

        grad_w_out = spread(hidden, dy_rows, far_hidden, far_dy)
        grad_w_in = spread(x_rows, d_pre, far_x, far_dpre)

        logits = jnp.dot(tokens, w_router, preferred_element_type=f32)
        router_prob = jax.nn.softmax(logits, axis=-1)
        chosen = expert_ids[:, None] == jnp.arange(n_experts)[None, :]
        gate_prob = jnp.sum(jnp.where(chosen, router_prob, 0.0), axis=1)
        slot_row = ((expert_ids % tp_size) * ep_size + expert_ids // tp_size) * cap + jnp.minimum(position, cap - 1)
        y_tok = jnp.where(kept[:, None], jnp.take(y_all, slot_row, axis=0, mode="clip"), 0)
        dx_moe = jnp.where(kept[:, None], jnp.take(s_all, slot_row, axis=0, mode="clip"), 0)
        moe_out = (gate_prob[:, None] * y_tok.astype(f32)).astype(bf16)
        d_gate = jnp.sum(grad_out.astype(f32) * y_tok.astype(f32), axis=1)
        d_logits = (d_gate[:, None] * router_prob * (chosen.astype(f32) - gate_prob[:, None])).astype(bf16)
        router_grad = jnp.einsum("te,de->td", d_logits, w_router, preferred_element_type=f32)
        grad_tokens = (dx_moe.astype(f32) + router_grad).astype(bf16)
        grad_w_router = lax.psum(jnp.einsum("td,te->de", tokens, d_logits, preferred_element_type=f32), "ep")
        return moe_out, grad_tokens, grad_w_in, grad_w_out, grad_w_router

    in_specs = (row_spec, row_spec, P(None, None), P("ep", None, "tp"), P("ep", "tp", None), P(("dp", "ep")))
    out_specs = (row_spec, row_spec, P(("dp", "ep"), None, "tp"), P(("dp", "ep"), "tp", None), P("dp", None))
    return jax.shard_map(block, mesh=mesh, in_specs=in_specs, out_specs=out_specs, check_vma=False)
```

time: 2050 us -> 783 us (0.38)
  blocking collectives: 1010 us -> 148 us
  local copies, waits for them, and re-layouts: 416 us -> 189 us
  waiting for transfers between devices: 298 us -> 144 us
  other arithmetic: 79.8 us -> 27.8 us
  matrix products: 184 us -> 217 us
    psum x1 -> x0, blocking collectives: 1010 us -> none  [local_block(): y_rows = lax.psum(y_part, 'tp').astype(jnp.bfloat16)]
    all_to_all x4 -> x3, waiting for transfers between devices: 298 us -> 3.33 us  [exchange(): lax.all_to_all(rows.reshape(ep_size, cap, rows.shape[1]), 'ep', 0, 0, til...]
    reshape x8 -> x0, local copies, waits for them, and re-layouts: 201 us -> none  [the longest x4 86.6 us: dispatch(): slot_buf[:n_slots].reshape(ep_size, local_experts, capacity, d_model)]
    all_to_all x0 -> x3, blocking collectives: none -> 148 us  [exchange(): lax.all_to_all(rows.reshape(ep_size, cap, rows.shape[1]), 'ep', 0, 0, til...]
    ppermute x0 -> x10, waiting for transfers between devices: none -> 141 us  [the longest x2 73.2 us: spread(): lax.ppermute(nxt, 'tp', [(i, (i + 1) % tp_size) for i in range(tp_size)])]
    gather x2 -> x6, local copies, waits for them, and re-layouts: 88.6 us -> 157 us  [the longest x1 46.4 us: block(): jnp.take(y_all, slot_row, axis=0, mode='clip')]
    scatter x1 -> x0, other arithmetic: 47.9 us -> none  [dispatch(): jnp.zeros((n_slots + 1, d_model), rows.dtype).at[slot_index].set(rows)]
    scatter x1 -> x0, local copies, waits for them, and re-layouts: 45.3 us -> none  [dispatch(): jnp.zeros((n_slots + 1, d_model), rows.dtype).at[slot_index].set(rows)]
  transfers between devices with their start and end apart: 5 -> 16, of which waited for: 4 -> 6; matrix products, arithmetic and copies ran while one was open for 23% -> 50% of each run, Pallas kernels for 0% -> 0%
where the time goes in v1:
time: 783 us; the launch traced here: 774 us
  matrix products  217 us (28%)
  local copies, waits for them, and re-layouts  189 us (24%)
  blocking collectives  148 us (19%)
  waiting for transfers between devices  144 us (18%)
  starting transfers between devices  33.3 us (4%)
  other arithmetic  27.8 us (4%)
  between operations  14.7 us (2%)
    all_to_all x3, blocking collectives, exchange(): lax.all_to_all(rows.reshape(ep_size, cap, rows.shape[1]), 'ep', 0, 0, til...  148 us
    ppermute x2, waiting for transfers between devices, spread(): lax.ppermute(nxt, 'tp', [(i, (i + 1) % tp_size) for i in range(tp_size)])  73.2 us
    dot_general x8, matrix products, rows_product(): lax.dot_general(left, right, (((0,), (0,)), ((), ())), preferred_element_...  72.1 us
    ppermute x6, waiting for transfers between devices, from_offset(): lax.ppermute(mine, 'tp', [(i, (i - offset) % tp_size) for i in range(tp_s...  67.7 us
    gather x1, local copies, waits for them, and re-layouts, block(): jnp.take(y_all, slot_row, axis=0, mode='clip')  46.4 us
    gather x1, local copies, waits for them, and re-layouts, block(): jnp.take(s_all, slot_row, axis=0, mode='clip')  44.4 us
    dot_general x1, matrix products, block(): jnp.einsum('rd,kfd->krf', dy_rows, wo, preferred_element_type=f32)  38.2 us
    gather x2, local copies, waits for them, and re-layouts, send_rows(): gy_send = jnp.take(grad_out, slot_token, axis=0, mode='clip')  33.1 us
  transfers between devices with their start and end apart: 16, of which 6 were waited for; matrix products, arithmetic and copies ran while one was open for 50% of the time, Pallas kernels for 0%

profile of v1, /device:TPU:97, one launch (start us, length us, event | category | flops | bytes accessed | tf_op | source)
XLA Modules:
  0.0 773.7 jit_solution(24091836688751507)
XLA Ops:
  17.5 16.5 %gather_fusion = bf16[2496,768]{1,0:T(8,128)(2,1)} fusion(bf16[8192,768]{1,0:T(8,128)(2,1)} %param.6, s32[3072]{0:T(1024)S(1)} %pad_clamp_fusion.1), kind=kCustom, calls=%fused_computation | custom fusion | bytes 7677696 | tf_op jit(solution)/shard_map/jit(_take)/gather | solution.py:64
  34.0 6.5 all-to-all-start
  53.3 20.2 %collective-permute-done.2 = bf16[768,768]{1,0:T(8,128)(2,1)S(1)} collective-permute-done((bf16[768,768]{1,0:T(8,128)(2,1)S(1)}, bf16[768,768]{1,0:T(8,128)(2,1)S(1)}, u32[]{:S(2)}, u32[]{:S(2)}) %collective-permute-start.2) | collective-permute-done | bytes 1179680 | tf_op jit(solution)/shard_map/ppermute | solution.py:24
  76.1 23.7 %collective-permute-done = bf16[768,768]{1,0:T(8,128)(2,1)} collective-permute-done((bf16[768,768]{1,0:T(8,128)(2,1)S(1)}, bf16[768,768]{1,0:T(8,128)(2,1)}, u32[]{:S(2)}, u32[]{:S(2)}) %collective-permute-start) | collective-permute-done | bytes 1179680 | tf_op jit(solution)/shard_map/ppermute | solution.py:24
  99.8 26.8 %fusion.10 = (bf16[4,2496,768]{2,1,0:T(8,128)(2,1)}, f32[4,768,2496]{1,2,0:T(8,128)}) fusion(bf16[2496,768,1]{1,0,2:T(8,128)(2,1)} %bitcast.9, bf16[1,768,768]{2,1,0:T(8,128)(2,1)} %bitcast.161, bf16[1,768,768]{2,1,0:T(8,128)(2,1)} %bitcast.163, bf16[1,768,768]{2,1,0:T(8,128)(2,1)S(1)} %get-tuple-element.17, bf16[1,768,768]{2,1,0:T(8,128)(2,1)} %bitcast.2), kind=kOutput, calls=%fused_computation.23 | convolution fusion | flops 11865489408 | bytes 54558720 | tf_op jit(solution)/shard_map/rd,kdf->krf/dot_general | solution.py:77
  126.6 23.7 %collective-permute-done.3 = bf16[768,768]{1,0:T(8,128)(2,1)} collective-permute-done((bf16[768,768]{1,0:T(8,128)(2,1)}, bf16[768,768]{1,0:T(8,128)(2,1)}, u32[]{:S(2)}, u32[]{:S(2)}) %collective-permute-start.3) | collective-permute-done | bytes 1179680 | tf_op jit(solution)/shard_map/ppermute | solution.py:24
  150.3 15.9 %bitcast_convert_fusion.1 = bf16[2496,768]{1,0:T(8,128)(2,1)S(1)} fusion(bf16[4,2496,768]{2,1,0:T(8,128)(2,1)} %get-tuple-element.29, bf16[1,768,768]{2,1,0:T(8,128)(2,1)} %bitcast.16, bf16[1,768,768]{2,1,0:T(8,128)(2,1)} %bitcast.14, bf16[1,768,768]{2,1,0:T(8,128)(2,1)S(1)} %get-tuple-element.13, bf16[1,768,768]{2,1,0:T(8,128)(2,1)} %bitcast.12), kind=kOutput, calls=%fused_computation.45 | convolution fusion | flops 11786600448 | bytes 23887872 | tf_op jit(solution)/shard_map/krf,kfd->rd/dot_general | solution.py:80
  166.2 50.4 %all_to_all.30 = bf16[8,312,768]{2,1,0:T(8,128)(2,1)} all-to-all(bf16[8,312,768]{2,1,0:T(8,128)(2,1)S(1)} %bitcast.158), channel_id=1, replica_groups=mesh['dp'=1,'tp'=4,'ep'=8] {'ep'}, dimensions={0} | all-to-all | bytes 7667712 | tf_op jit(solution)/shard_map/all_to_all | solution.py:60
  216.7 16.5 %gather_fusion.2 = bf16[2496,768]{1,0:T(8,128)(2,1)} fusion(bf16[8192,768]{1,0:T(8,128)(2,1)} %param.7, s32[3072]{0:T(1024)S(1)} %pad_clamp_fusion.1), kind=kCustom, calls=%fused_computation.2 | custom fusion | bytes 7677696 | tf_op jit(solution)/shard_map/jit(_take)/gather | solution.py:65
  239.9 49.0 %all_to_all.31 = bf16[8,312,768]{2,1,0:T(8,128)(2,1)S(1)} all-to-all(bf16[8,312,768]{2,1,0:T(8,128)(2,1)S(1)} %fusion.23), channel_id=1, replica_groups=mesh['dp'=1,'tp'=4,'ep'=8] {'ep'}, dimensions={0} | all-to-all | bytes 7667712 | tf_op jit(solution)/shard_map/all_to_all | solution.py:60
  288.9 38.2 %fusion.6 = bf16[4,2496,768]{2,1,0:T(8,128)(2,1)} fusion(f32[4,768,2496]{1,2,0:T(8,128)} %get-tuple-element.30, bf16[2496,768,1]{1,0,2:T(8,128)(2,1)S(1)} %bitcast.153, bf16[1,768,768]{2,1,0:T(8,128)(2,1)} %bitcast.16, bf16[1,768,768]{2,1,0:T(8,128)(2,1)} %bitcast.14, bf16[1,768,768]{2,1,0:T(8,128)(2,1)} %copy-done.6, bf16[1,768,768]{2,1,0:T(8,128)(2,1)} %bitcast.12), kind=kOutput, calls=%fused_computation.16 | convolution fusion | flops 11938037760 | bytes 54558720 | tf_op jit(solution)/shard_map/rd,kfd->krf/dot_general | solution.py:84
  327.1 16.7 %bitcast_convert_fusion = bf16[2496,768]{1,0:T(8,128)(2,1)S(1)} fusion(bf16[4,2496,768]{2,1,0:T(8,128)(2,1)} %fusion.6, bf16[1,768,768]{2,1,0:T(8,128)(2,1)} %bitcast.162, bf16[1,768,768]{2,1,0:T(8,128)(2,1)} %bitcast.164, bf16[1,768,768]{2,1,0:T(8,128)(2,1)S(1)} %get-tuple-element.17, bf16[1,768,768]{2,1,0:T(8,128)(2,1)} %bitcast.2), kind=kOutput, calls=%fused_computation.44 | convolution fusion | flops 11786600448 | bytes 23887872 | tf_op jit(solution)/shard_map/krf,kdf->rd/dot_general | solution.py:86
  343.8 49.1 %all_to_all.32 = bf16[8,312,768]{2,1,0:T(8,128)(2,1)} all-to-all(bf16[8,312,768]{2,1,0:T(8,128)(2,1)S(1)} %bitcast.157), channel_id=1, replica_groups=mesh['dp'=1,'tp'=4,'ep'=8] {'ep'}, dimensions={0} | all-to-all | bytes 7667712 | tf_op jit(solution)/shard_map/all_to_all | solution.py:60
  393.2 16.5 %gather_fusion.4 = bf16[2496,768]{1,0:T(8,128)(2,1)} fusion(bf16[8192,768]{1,0:T(8,128)(2,1)} %param.6, s32[3072]{0:T(1024)S(1)} %pad_clamp_fusion), kind=kCustom, calls=%fused_computation.4 | custom fusion | bytes 7677696 | tf_op jit(solution)/shard_map/jit(_take)/gather | solution.py:64
  415.6 16.6 %gather_fusion.5 = bf16[2496,768]{1,0:T(8,128)(2,1)} fusion(bf16[8192,768]{1,0:T(8,128)(2,1)} %param.7, s32[3072]{0:T(1024)S(1)} %pad_clamp_fusion), kind=kCustom, calls=%fused_computation.5 | custom fusion | bytes 7677696 | tf_op jit(solution)/shard_map/jit(_take)/gather | solution.py:65
  436.1 8.6 %fusion.116 = (f32[8192]{0:T(1024)S(1)}, f32[8192,32]{0,1:T(8,128)S(1)}) fusion(bf16[8192,768]{1,0:T(8,128)(2,1)} %param.6, bf16[768,32]{0,1:T(8,128)(2,1)S(1)} %copy-done), kind=kOutput, calls=%fused_computation.203 | convolution fusion | flops 402907136 | bytes 13713408 | tf_op jit(solution)/shard_map/dot_general | solution.py:116
  449.0 8.1 %fusion.30 = f32[768,768]{1,0:T(8,128)} fusion(bf16[2496,768]{1,0:T(8,128)(2,1)} %bitcast.8, bf16[4,2496,768]{2,1,0:T(8,128)(2,1)} %fusion.6), kind=kOutput, calls=%fused_computation.60 | convolution fusion | flops 2944401408 | bytes 10027008 | tf_op jit(solution)/shard_map/dot_general | solution.py:101
  466.2 8.1 %fusion.29 = f32[768,768]{1,0:T(8,128)} fusion(bf16[2496,768]{1,0:T(8,128)(2,1)} %bitcast.8, bf16[4,2496,768]{2,1,0:T(8,128)(2,1)} %fusion.6), kind=kOutput, calls=%fused_computation.58 | convolution fusion | flops 2944401408 | bytes 10027008 | tf_op jit(solution)/shard_map/dot_general | solution.py:101
  477.0 6.8 fusion.27
  483.8 6.9 fusion.26
  493.5 8.7 %fusion.37 = f32[2496,768]{1,0:T(8,128)} fusion(bf16[2496,768]{1,0:T(8,128)(2,1)} %bitcast.30, bf16[4,768,768]{2,1,0:T(8,128)(2,1)} %param.9, s32[]{:T(128)S(6)} %select_n.222), kind=kOutput, calls=%fused_computation.73 | convolution fusion | flops 2944401408 | bytes 12681220 | tf_op jit(solution)/shard_map/dot_general | solution.py:94
  506.8 7.9 %bitcast_dynamic-update-slice_fusion.7 = f32[4,768,768]{2,1,0:T(8,128)} fusion(f32[4,768,768]{2,1,0:T(8,128)} %broadcast.197.clone, s32[]{:T(128)S(6)} %select_n.214, bf16[2496,768]{1,0:T(8,128)(2,1)} %bitcast.8, bf16[4,2496,768]{2,1,0:T(8,128)(2,1)} %fusion.6), kind=kOutput, calls=%fused_computation.72 | convolution fusion | flops 2944401408 | bytes 10027012 | tf_op jit(solution)/shard_map/dot_general | solution.py:101
  514.8 20.0 %bitcast_dynamic-update-slice_fusion.6 = f32[4,768,768]{2,1,0:T(8,128)} fusion(f32[4,768,768]{2,1,0:T(8,128)} %bitcast_dynamic-update-slice_fusion.7, s32[]{:T(128)S(6)} %select_n.222, bf16[2496,768]{1,0:T(8,128)(2,1)} %bitcast.30, f32[2496,768]{1,0:T(8,128)} %fusion.37, bf16[2496,768]{1,0:T(8,128)(2,1)} %bitcast.32, bf16[4,768,768]{2,1,0:T(8,128)(2,1)} %param.10), kind=kOutput, calls=%fused_computation.71 | convolution fusion | flops 5927141376 | bytes 18875392 | tf_op jit(solution)/shard_map/dot_general | solution.py:101
  540.3 6.9 bitcast_dynamic-update-slice_fusion.3
  547.3 7.4 bitcast_dynamic-update-slice_fusion.2
  554.6 25.0 %collective-permute-done.6 = f32[768,768]{1,0:T(8,128)} collective-permute-done((f32[768,768]{1,0:T(8,128)}, f32[768,768]{1,0:T(8,128)}, u32[]{:S(2)}, u32[]{:S(2)}) %collective-permute-start.6) | collective-permute-done | bytes 2359328 | tf_op jit(solution)/shard_map/ppermute | solution.py:106
  582.8 48.2 %collective-permute-done.8 = f32[768,768]{1,0:T(8,128)} collective-permute-done((f32[768,768]{1,0:T(8,128)}, f32[768,768]{1,0:T(8,128)}, u32[]{:S(2)}, u32[]{:S(2)}) %collective-permute-start.8) | collective-permute-done | bytes 2359328 | tf_op jit(solution)/shard_map/ppermute | solution.py:106
  639.1 46.4 %gather_fusion.1 = bf16[8192,768]{1,0:T(8,128)(2,1)} fusion(bf16[9984,768]{1,0:T(8,128)(2,1)} %all-gather.3.cloned.1.call-done, s32[8192]{0:T(1024)} %get-tuple-element.27), kind=kCustom, calls=%fused_computation.1 | custom fusion | bytes 25198592 | tf_op jit(solution)/shard_map/jit(_take)/gather | solution.py:121
  685.5 16.7 %fusion.12 = (f32[8192]{0:T(1024)S(1)}, bf16[8192,768]{1,0:T(8,128)(2,1)}) fusion(bf16[8192,768]{1,0:T(8,128)(2,1)} %param.7, bf16[8192,768]{1,0:T(8,128)(2,1)} %gather_fusion.1, pred[8192]{0:T(1024)(128)(4,1)S(1)} %copy-done.13, f32[8192]{0:T(1024)S(1)} %copy-done.7), kind=kLoop, calls=%fused_computation.25 | loop fusion | flops 44032000 | bytes 37822464 | tf_op jit(solution)/shard_map/reduce_sum | solution.py:124
  702.1 7.4 convolution_bitcast_fusion
  709.7 44.4 %gather_fusion.3 = bf16[8192,768]{1,0:T(8,128)(2,1)} fusion(bf16[9984,768]{1,0:T(8,128)(2,1)} %all-gather.5.cloned.1.call-done, s32[8192]{0:T(1024)S(1)} %copy-done.10), kind=kCustom, calls=%fused_computation.3 | custom fusion | bytes 25198592 | tf_op jit(solution)/shard_map/jit(_take)/gather | solution.py:122
  754.1 11.1 %add_convert_fusion = bf16[8192,768]{1,0:T(8,128)(2,1)} fusion(bf16[8192,768]{1,0:T(8,128)(2,1)} %gather_fusion.3, pred[8192]{0:T(1024)(128)(4,1)S(1)} %copy-done.13, bf16[768,32]{0,1:T(8,128)(2,1)S(1)} %copy-done, f32[8192]{0:T(1024)S(1)} %copy-done.7, f32[8192]{0:T(1024)S(1)} %get-tuple-element.9, s32[8192]{0:T(1024)S(1)} %copy-done.5, ...), kind=kOutput, calls=%fused_computation.26 | convolution fusion | flops 429916160 | bytes 26435584 | tf_op jit(solution)/shard_map/te,de->td/dot_general | solution.py:126
  (130 shorter events, 84.0 us)
Async XLA Ops:
  7.2 226.2 %copy-start = (bf16[768,32]{0,1:T(8,128)(2,1)S(1)}, bf16[768,32]{0,1:T(8,128)(2,1)}, u32[]{:S(2)}) copy-start(bf16[768,32]{0,1:T(8,128)(2,1)} %param.8) | copy-start | bytes 147460
  34.0 14.6 %slice-start = ((s8[4718592]{0:T(1024)(128)(4,1)}), s8[524288]{0:T(1024)(128)(4,1)S(1)}, s32[]{:S(2)}) async-start(s8[4718592]{0:T(1024)(128)(4,1)} %bitcast.151), calls=%async_computation.9 | async-start | bytes 1048576
  34.0 65.8 %all-to-all-start = ((bf16[8,312,768]{2,1,0:T(8,128)(2,1)}), bf16[8,312,768]{2,1,0:T(8,128)(2,1)}, u32[]{:S(2)}, u32[]{:S(2)}) async-start(bf16[8,312,768]{2,1,0:T(8,128)(2,1)} %bitcast.145), calls=%async_computation | async-start | bytes 7667712 | tf_op jit(solution)/shard_map/all_to_all | solution.py:60
  40.5 598.5 %all-gather.3.cloned.1.call-start = ((), (), s32[]{:S(2)}) async-start(), calls=%async_computation.6 | async-start | bytes 19169280 | tf_op jit(solution)/shard_map/all_gather | solution.py:82
  40.5 8.0 %slice-start.1 = ((s8[4718592]{0:T(1024)(128)(4,1)}), s8[4194304]{0:T(1024)(128)(4,1)S(1)}, s32[]{:S(2)}) async-start(s8[4718592]{0:T(1024)(128)(4,1)} %bitcast.151), calls=%async_computation.10 | async-start | bytes 8388608
  43.3 30.3 %collective-permute-start.2 = (bf16[768,768]{1,0:T(8,128)(2,1)S(1)}, bf16[768,768]{1,0:T(8,128)(2,1)S(1)}, u32[]{:S(2)}, u32[]{:S(2)}) collective-permute-start(bf16[768,768]{1,0:T(8,128)(2,1)S(1)} %get-tuple-element.18), channel_id=1, source_target_pairs={{0,8},{8,16},{16,24},{24,0},{1,9},{9,17},{17,25},{25,1},{2,10},{10... | collective-permute-start | bytes 3538952 | tf_op jit(solution)/shard_map/ppermute | solution.py:24
  44.8 30.2 %collective-permute-start.1 = (bf16[768,768]{1,0:T(8,128)(2,1)S(1)}, bf16[768,768]{1,0:T(8,128)(2,1)S(1)}, u32[]{:S(2)}, u32[]{:S(2)}) collective-permute-start(bf16[768,768]{1,0:T(8,128)(2,1)S(1)} %get-tuple-element.16), channel_id=1, source_target_pairs={{0,24},{8,0},{16,8},{24,16},{1,25},{9,1},{17,9},{25,17},{2,26},{10... | collective-permute-start | bytes 3538952 | tf_op jit(solution)/shard_map/ppermute | solution.py:24
  47.5 52.3 %collective-permute-start = (bf16[768,768]{1,0:T(8,128)(2,1)S(1)}, bf16[768,768]{1,0:T(8,128)(2,1)}, u32[]{:S(2)}, u32[]{:S(2)}) collective-permute-start(bf16[768,768]{1,0:T(8,128)(2,1)S(1)} %get-tuple-element.15), channel_id=1, source_target_pairs={{0,16},{8,24},{16,0},{24,8},{1,17},{9,25},{17,1},{25,9},{2,18},{10... | collective-permute-start | bytes 3538952 | tf_op jit(solution)/shard_map/ppermute | solution.py:24
  50.5 99.9 %copy-start.6 = (bf16[1,768,768]{2,1,0:T(8,128)(2,1)}, bf16[1,768,768]{2,1,0:T(8,128)(2,1)S(1)}, u32[]{:S(2)}) copy-start(bf16[1,768,768]{2,1,0:T(8,128)(2,1)S(1)} %get-tuple-element.13) | copy-start | bytes 3538948
  50.5 76.2 %collective-permute-start.5 = (bf16[768,768]{1,0:T(8,128)(2,1)}, bf16[768,768]{1,0:T(8,128)(2,1)}, u32[]{:S(2)}, u32[]{:S(2)}) collective-permute-start(bf16[768,768]{1,0:T(8,128)(2,1)} %get-tuple-element.14), channel_id=1, source_target_pairs={{0,8},{8,16},{16,24},{24,0},{1,9},{9,17},{17,25},{25,1},{2,10},{10... | collective-permute-start | bytes 3538952 | tf_op jit(solution)/shard_map/ppermute | solution.py:24
  51.3 75.3 %collective-permute-start.4 = (bf16[768,768]{1,0:T(8,128)(2,1)}, bf16[768,768]{1,0:T(8,128)(2,1)}, u32[]{:S(2)}, u32[]{:S(2)}) collective-permute-start(bf16[768,768]{1,0:T(8,128)(2,1)} %get-tuple-element.12), channel_id=1, source_target_pairs={{0,24},{8,0},{16,8},{24,16},{1,25},{9,1},{17,9},{25,17},{2,26},{10... | collective-permute-start | bytes 3538952 | tf_op jit(solution)/shard_map/ppermute | solution.py:24
  73.6 76.8 %collective-permute-start.3 = (bf16[768,768]{1,0:T(8,128)(2,1)}, bf16[768,768]{1,0:T(8,128)(2,1)}, u32[]{:S(2)}, u32[]{:S(2)}) collective-permute-start(bf16[768,768]{1,0:T(8,128)(2,1)} %get-tuple-element.11), channel_id=1, source_target_pairs={{0,16},{8,24},{16,0},{24,8},{1,17},{9,25},{17,1},{25,9},{2,18},{10... | collective-permute-start | bytes 3538952 | tf_op jit(solution)/shard_map/ppermute | solution.py:24
  216.7 493.0 %all-gather.5.cloned.1.call-start = ((), (), s32[]{:S(2)}) async-start(), calls=%async_computation.7 | async-start | bytes 19169280 | tf_op jit(solution)/shard_map/all_gather | solution.py:88
  288.9 38.2 %copy-start.2 = (bf16[8,312,768]{2,1,0:T(8,128)(2,1)}, bf16[8,312,768]{2,1,0:T(8,128)(2,1)S(1)}, u32[]{:S(2)}) copy-start(bf16[8,312,768]{2,1,0:T(8,128)(2,1)S(1)} %all_to_all.31) | copy-start | bytes 11501572
  343.8 49.2 %copy-start.12 = (f32[24,312]{1,0:T(8,128)S(1)}, f32[24,312]{1,0:T(8,128)}, u32[]{:S(2)}) copy-start(f32[24,312]{1,0:T(8,128)} %copy-done.11) | copy-start | bytes 89860
  343.8 49.2 %copy-start.16 = (s32[8]{0:T(128)S(1)}, s32[8]{0:T(128)}, u32[]{:S(2)}) copy-start(s32[8]{0:T(128)} %get-tuple-element.37) | copy-start | bytes 100
  409.7 50.8 %all-to-all-start.4 = ((bf16[8,312,768]{2,1,0:T(8,128)(2,1)}), bf16[8,312,768]{2,1,0:T(8,128)(2,1)}, u32[]{:S(2)}, u32[]{:S(2)}) async-start(bf16[8,312,768]{2,1,0:T(8,128)(2,1)} %bitcast.146), calls=%async_computation.4 | async-start | bytes 7667712 | tf_op jit(solution)/shard_map/all_to_all | solution.py:60
  415.6 16.6 %copy-start.15 = (s32[8]{0:T(128)S(1)}, s32[8]{0:T(128)}, u32[]{:S(2)}) copy-start(s32[8]{0:T(128)} %copy-done.14) | copy-start | bytes 100
  436.0 8.9 %copy-start.9 = (s32[4,2,8,128]{3,1,2,0:T(2,128)S(1)}, s32[4,2,8,128]{3,1,2,0:T(2,128)}, u32[]{:S(2)}) copy-start(s32[4,2,8,128]{3,1,2,0:T(2,128)} %copy-done.8) | copy-start | bytes 98308
  436.0 9.5 %copy-start.5 = (s32[8192]{0:T(1024)S(1)}, s32[8192]{0:T(1024)}, u32[]{:S(2)}) copy-start(s32[8192]{0:T(1024)} %param.11) | copy-start | bytes 98308
  436.1 10.4 %copy-start.1 = (bf16[2496,768]{1,0:T(8,128)(2,1)S(1)}, bf16[2496,768]{1,0:T(8,128)(2,1)}, u32[]{:S(2)}) copy-start(bf16[2496,768]{1,0:T(8,128)(2,1)} %gather_fusion.5) | copy-start | bytes 11501572
  460.5 54.3 %all-to-all-start.5 = ((bf16[8,312,768]{2,1,0:T(8,128)(2,1)}), bf16[8,312,768]{2,1,0:T(8,128)(2,1)}, u32[]{:S(2)}, u32[]{:S(2)}) async-start(bf16[8,312,768]{2,1,0:T(8,128)(2,1)} %fusion.22), calls=%async_computation.5 | async-start | bytes 7667712 | tf_op jit(solution)/shard_map/all_to_all | solution.py:60
  465.8 299.3 %all-reduce.2.cloned.1.call-start = ((), (), s32[]{:S(2)}) async-start(), calls=%async_computation.8 | async-start | bytes 196608 | tf_op jit(solution)/shard_map/psum | solution.py:128
  466.2 10.8 %copy-start.3 = (bf16[8,312,768]{2,1,0:T(8,128)(2,1)S(1)}, bf16[8,312,768]{2,1,0:T(8,128)(2,1)}, u32[]{:S(2)}) copy-start(bf16[8,312,768]{2,1,0:T(8,128)(2,1)} %copy-done.2) | copy-start | bytes 11501572
  474.3 105.2 %collective-permute-start.6 = (f32[768,768]{1,0:T(8,128)}, f32[768,768]{1,0:T(8,128)}, u32[]{:S(2)}, u32[]{:S(2)}) collective-permute-start(f32[768,768]{1,0:T(8,128)} %fusion.30), channel_id=1, source_target_pairs={{0,8},{8,16},{16,24},{24,0},{1,9},{9,17},{17,25},{25,1},{2,10},{10... | collective-permute-start | bytes 7077896 | tf_op jit(solution)/shard_map/ppermute | solution.py:106
  474.9 159.3 %collective-permute-start.7 = (f32[768,768]{1,0:T(8,128)}, f32[768,768]{1,0:T(8,128)S(1)}, u32[]{:S(2)}, u32[]{:S(2)}) collective-permute-start(f32[768,768]{1,0:T(8,128)} %fusion.29), channel_id=1, source_target_pairs={{0,24},{8,0},{16,8},{24,16},{1,25},{9,1},{17,9},{25,17},{2,26},{10... | collective-permute-start | bytes 7077896 | tf_op jit(solution)/shard_map/ppermute | solution.py:107
  483.8 147.2 %collective-permute-start.8 = (f32[768,768]{1,0:T(8,128)}, f32[768,768]{1,0:T(8,128)}, u32[]{:S(2)}, u32[]{:S(2)}) collective-permute-start(f32[768,768]{1,0:T(8,128)} %fusion.27), channel_id=1, source_target_pairs={{0,8},{8,16},{16,24},{24,0},{1,9},{9,17},{17,25},{25,1},{2,10},{10... | collective-permute-start | bytes 7077896 | tf_op jit(solution)/shard_map/ppermute | solution.py:106
  490.7 145.1 %collective-permute-start.9 = (f32[768,768]{1,0:T(8,128)}, f32[768,768]{1,0:T(8,128)}, u32[]{:S(2)}, u32[]{:S(2)}) collective-permute-start(f32[768,768]{1,0:T(8,128)} %fusion.26), channel_id=1, source_target_pairs={{0,24},{8,0},{16,8},{24,16},{1,25},{9,1},{17,9},{25,17},{2,26},{10... | collective-permute-start | bytes 7077896 | tf_op jit(solution)/shard_map/ppermute | solution.py:107
  534.7 12.5 %slice-start.2 = ((s8[7667712]{0:T(1024)(128)(4,1)}), s8[4194304]{0:T(1024)(128)(4,1)S(1)}, s32[]{:S(2)}) async-start(s8[7667712]{0:T(1024)(128)(4,1)} %bitcast.165), calls=%async_computation.11 | async-start | bytes 8388608
  639.0 46.4 %copy-start.7 = (f32[8192]{0:T(1024)S(1)}, f32[8192]{0:T(1024)}, u32[]{:S(2)}) copy-start(f32[8192]{0:T(1024)} %select_reduce_fusion.1) | copy-start | bytes 98308
  639.0 46.4 %copy-start.13 = (pred[8192]{0:T(1024)(128)(4,1)S(1)}, pred[8192]{0:T(1024)(128)(4,1)}, u32[]{:S(2)}) copy-start(pred[8192]{0:T(1024)(128)(4,1)} %broadcast_compare_fusion) | copy-start | bytes 24580
  702.1 7.5 copy-start.10
  (7 other events, 19.3 us)
Sparse Core Ops, SparseCore 0:
  216.8 137.6 all-gather.2
  393.1 190.1 all-gather.4
  709.8 50.1 all-reduce.1

commit v2 on v1

--- a/solution.py
+++ b/solution.py
@@ -10,8 +10,16 @@
     row_spec = P(("dp", "ep"), None)
     bf16, f32 = jnp.bfloat16, jnp.float32
 
+    def gelu_and_slope(a):
+        c, k = (2.0 / jnp.pi) ** 0.5, 0.044715
+        square = a * a
+        t = jnp.tanh(a * (c + (c * k) * square))
+        half = 0.5 + 0.5 * t
+        value = a * half
+        return value.astype(bf16), half + value * (1.0 - t) * (c + (3.0 * c * k) * square)
+
     def block(tokens, grad_out, w_router, w_in, w_out, expert_ids):
-        n_local, _ = tokens.shape
+        n_local, d_model = tokens.shape
         n_experts = w_router.shape[1]
         local_experts = w_in.shape[0]
         assert local_experts == tp_size == 4
@@ -27,7 +35,8 @@
             own = lax.dynamic_index_in_dim(weight, my_tp, 0, keepdims=False)
             return jnp.stack([from_offset(weight, 2), own, from_offset(weight, 1), from_offset(weight, 3)])
 
-        wi, wo = gather_weight(w_in), gather_weight(w_out)
+        wi = gather_weight(w_in)
+        wo = gather_weight(w_out)
 
         block = 256
         n_blocks = n_local // block
@@ -75,14 +84,16 @@
         dy_rows = exchange(dy_send)
 
         pre_act = jnp.einsum("rd,kdf->krf", x_rows, wi, preferred_element_type=f32)
-        act_val, act_vjp = jax.vjp(jax.nn.gelu, pre_act)
-        hidden = act_val.astype(bf16)
+        hidden, slope = gelu_and_slope(pre_act)
         y_rows = jnp.einsum("krf,kfd->rd", hidden, wo, preferred_element_type=f32).astype(bf16)
-        y_back = exchange(y_rows)
+        early = d_model // 3
+        y_early = lax.all_gather(y_rows[:, :early], "tp", axis=0, tiled=True).reshape(tp_size, ep_size, cap, early)
+        y_back = exchange(y_rows[:, early:])
         y_all = lax.all_gather(y_back, "tp", axis=0, tiled=True)
+        y_early = lax.all_to_all(y_early, "ep", 1, 1, tiled=True).reshape(-1, early)
 
         d_hidden = jnp.einsum("rd,kfd->krf", dy_rows, wo, preferred_element_type=f32)
-        d_pre = act_vjp(d_hidden)[0].astype(bf16)
+        d_pre = (d_hidden * slope).astype(bf16)
         d_slot = jnp.einsum("krf,kdf->rd", d_pre, wi, preferred_element_type=f32).astype(bf16)
         s_back = exchange(d_slot)
         s_all = lax.all_gather(s_back, "tp", axis=0, tiled=True)
@@ -92,10 +103,9 @@
         far_x = exchange(far_x)
         far_dy = exchange(far_dy)
         far_pre = jnp.dot(far_x, lax.dynamic_index_in_dim(w_in, far_tp, 0, keepdims=False), preferred_element_type=f32)
-        far_act, far_vjp = jax.vjp(jax.nn.gelu, far_pre)
-        far_hidden = far_act.astype(bf16)
+        far_hidden, far_slope = gelu_and_slope(far_pre)
         far_dh = lax.dot_general(far_dy, lax.dynamic_index_in_dim(w_out, far_tp, 0, keepdims=False), (((1,), (1,)), ((), ())), preferred_element_type=f32)
-        far_dpre = far_vjp(far_dh)[0].astype(bf16)
+        far_dpre = (far_dh * far_slope).astype(bf16)
 
         def rows_product(left, right):
             return lax.dot_general(left, right, (((0,), (0,)), ((), ())), preferred_element_type=f32)
@@ -118,12 +128,13 @@
         chosen = expert_ids[:, None] == jnp.arange(n_experts)[None, :]
         gate_prob = jnp.sum(jnp.where(chosen, router_prob, 0.0), axis=1)
         slot_row = ((expert_ids % tp_size) * ep_size + expert_ids // tp_size) * cap + jnp.minimum(position, cap - 1)
+        y_all = jnp.concatenate([y_early, y_all], axis=1)
         y_tok = jnp.where(kept[:, None], jnp.take(y_all, slot_row, axis=0, mode="clip"), 0)
         dx_moe = jnp.where(kept[:, None], jnp.take(s_all, slot_row, axis=0, mode="clip"), 0)
         moe_out = (gate_prob[:, None] * y_tok.astype(f32)).astype(bf16)
         d_gate = jnp.sum(grad_out.astype(f32) * y_tok.astype(f32), axis=1)
         d_logits = (d_gate[:, None] * router_prob * (chosen.astype(f32) - gate_prob[:, None])).astype(bf16)
-        router_grad = jnp.einsum("te,de->td", d_logits, w_router, preferred_element_type=f32)
+        router_grad = lax.dot_general(d_logits, w_router, (((1,), (1,)), ((), ())), preferred_element_type=f32)
         grad_tokens = (dx_moe.astype(f32) + router_grad).astype(bf16)
         grad_w_router = lax.psum(jnp.einsum("td,te->de", tokens, d_logits, preferred_element_type=f32), "ep")
         return moe_out, grad_tokens, grad_w_in, grad_w_out, grad_w_router

time: 783 us -> 784 us (level)
  blocking collectives: 148 us -> 134 us
  local copies, waits for them, and re-layouts: 189 us -> 202 us
  other arithmetic: 27.8 us -> 40.8 us
  waiting for transfers between devices: 144 us -> 134 us
    all_to_all x3, blocking collectives: 148 us -> 134 us  [exchange(): lax.all_to_all(rows.reshape(ep_size, cap, rows.shape[1]), 'ep', 0, 0, til...]
    concatenate x0 -> x1, other arithmetic: none -> 13.1 us  [block(): y_all = jnp.concatenate([y_early, y_all], axis=1)]
    ppermute x2, waiting for transfers between devices: 73.2 us -> 61.8 us  [spread(): lax.ppermute(nxt, 'tp', [(i, (i + 1) % tp_size) for i in range(tp_size)])]
  transfers between devices with their start and end apart: 16 -> 18, of which waited for: 6 -> 6; matrix products, arithmetic and copies ran while one was open for 50% -> 52% of each run, Pallas kernels for 0% -> 0%
where the time goes in v2:
time: 784 us; the launch traced here: 775 us
  matrix products  210 us (27%)
  local copies, waits for them, and re-layouts  202 us (26%)
  waiting for transfers between devices  134 us (17%)
  blocking collectives  134 us (17%)
  other arithmetic  40.8 us (5%)
  starting transfers between devices  40.3 us (5%)
  between operations  14.7 us (2%)
    all_to_all x3, blocking collectives, exchange(): lax.all_to_all(rows.reshape(ep_size, cap, rows.shape[1]), 'ep', 0, 0, til...  134 us
    dot_general x8, matrix products, rows_product(): lax.dot_general(left, right, (((0,), (0,)), ((), ())), preferred_element_...  71.8 us
    ppermute x6, waiting for transfers between devices, from_offset(): lax.ppermute(mine, 'tp', [(i, (i - offset) % tp_size) for i in range(tp_s...  68.6 us
    ppermute x2, waiting for transfers between devices, spread(): lax.ppermute(nxt, 'tp', [(i, (i + 1) % tp_size) for i in range(tp_size)])  61.8 us
    gather x1, local copies, waits for them, and re-layouts, block(): jnp.take(y_all, slot_row, axis=0, mode='clip')  44.4 us
    gather x1, local copies, waits for them, and re-layouts, block(): jnp.take(s_all, slot_row, axis=0, mode='clip')  44.4 us
    gather x2, local copies, waits for them, and re-layouts, send_rows(): gy_send = jnp.take(grad_out, slot_token, axis=0, mode='clip')  33.2 us
    gather x2, local copies, waits for them, and re-layouts, send_rows(): x_send = jnp.take(tokens, slot_token, axis=0, mode='clip')  33 us
  transfers between devices with their start and end apart: 18, of which 6 were waited for; matrix products, arithmetic and copies ran while one was open for 52% of the time, Pallas kernels for 0%

profile of v2, /device:TPU:97, one launch (start us, length us, event | category | flops | bytes accessed | tf_op | source)
XLA Modules:
  0.0 775.4 jit_solution(12532918174932252139)
XLA Ops:
  17.4 16.5 %gather_fusion = bf16[2496,768]{1,0:T(8,128)(2,1)} fusion(bf16[8192,768]{1,0:T(8,128)(2,1)} %param.6, s32[3072]{0:T(1024)S(1)} %pad_clamp_fusion.1), kind=kCustom, calls=%fused_computation | custom fusion | bytes 7677696 | tf_op jit(solution)/shard_map/jit(_take)/gather | solution.py:73
  53.3 20.2 %collective-permute-done.2 = bf16[768,768]{1,0:T(8,128)(2,1)S(1)} collective-permute-done((bf16[768,768]{1,0:T(8,128)(2,1)S(1)}, bf16[768,768]{1,0:T(8,128)(2,1)S(1)}, u32[]{:S(2)}, u32[]{:S(2)}) %collective-permute-start.2) | collective-permute-done | bytes 1179680 | tf_op jit(solution)/shard_map/ppermute | solution.py:32
  76.1 23.7 %collective-permute-done = bf16[768,768]{1,0:T(8,128)(2,1)} collective-permute-done((bf16[768,768]{1,0:T(8,128)(2,1)S(1)}, bf16[768,768]{1,0:T(8,128)(2,1)}, u32[]{:S(2)}, u32[]{:S(2)}) %collective-permute-start) | collective-permute-done | bytes 1179680 | tf_op jit(solution)/shard_map/ppermute | solution.py:32
  99.7 25.8 %fusion.2 = (bf16[4,2496,768]{2,1,0:T(8,128)(2,1)}, f32[4,768,2496]{1,2,0:T(8,128)}) fusion(bf16[2496,768,1]{1,0,2:T(8,128)(2,1)} %bitcast.9, bf16[1,768,768]{2,1,0:T(8,128)(2,1)} %bitcast.159, bf16[1,768,768]{2,1,0:T(8,128)(2,1)} %bitcast.161, bf16[1,768,768]{2,1,0:T(8,128)(2,1)S(1)} %get-tuple-element.17, bf16[1,768,768]{2,1,0:T(8,128)(2,1)} %bitcast.2), kind=kOutput, calls=%fused_computation.15 | convolution fusion | flops 11857821696 | bytes 54558720 | tf_op jit(solution)/shard_map/rd,kdf->krf/dot_general | solution.py:86
  125.6 24.7 %collective-permute-done.3 = bf16[768,768]{1,0:T(8,128)(2,1)} collective-permute-done((bf16[768,768]{1,0:T(8,128)(2,1)}, bf16[768,768]{1,0:T(8,128)(2,1)}, u32[]{:S(2)}, u32[]{:S(2)}) %collective-permute-start.3) | collective-permute-done | bytes 1179680 | tf_op jit(solution)/shard_map/ppermute | solution.py:32
  150.3 15.9 %bitcast_convert_fusion.1 = bf16[2496,768]{1,0:T(8,128)(2,1)S(1)} fusion(bf16[4,2496,768]{2,1,0:T(8,128)(2,1)} %get-tuple-element.29, bf16[1,768,768]{2,1,0:T(8,128)(2,1)} %bitcast.16, bf16[1,768,768]{2,1,0:T(8,128)(2,1)} %bitcast.14, bf16[1,768,768]{2,1,0:T(8,128)(2,1)S(1)} %get-tuple-element.13, bf16[1,768,768]{2,1,0:T(8,128)(2,1)} %bitcast.12), kind=kOutput, calls=%fused_computation.29 | convolution fusion | flops 11786600448 | bytes 23887872 | tf_op jit(solution)/shard_map/krf,kfd->rd/dot_general | solution.py:88
  171.0 36.6 %all_to_all.35 = bf16[8,312,512]{2,1,0:T(8,128)(2,1)} all-to-all(bf16[8,312,512]{2,1,0:T(8,128)(2,1)S(1)} %bitcast.148), channel_id=1, replica_groups=mesh['dp'=1,'tp'=4,'ep'=8] {'ep'}, dimensions={0} | all-to-all | bytes 5111808 | tf_op jit(solution)/shard_map/all_to_all | solution.py:69
  208.1 16.6 %gather_fusion.2 = bf16[2496,768]{1,0:T(8,128)(2,1)} fusion(bf16[8192,768]{1,0:T(8,128)(2,1)} %param.7, s32[3072]{0:T(1024)S(1)} %pad_clamp_fusion.1), kind=kCustom, calls=%fused_computation.2 | custom fusion | bytes 7677696 | tf_op jit(solution)/shard_map/jit(_take)/gather | solution.py:74
  231.3 48.5 %all_to_all.36 = bf16[8,312,768]{2,1,0:T(8,128)(2,1)S(1)} all-to-all(bf16[8,312,768]{2,1,0:T(8,128)(2,1)S(1)} %fusion.8), channel_id=1, replica_groups=mesh['dp'=1,'tp'=4,'ep'=8] {'ep'}, dimensions={0} | all-to-all | bytes 7667712 | tf_op jit(solution)/shard_map/all_to_all | solution.py:69
  279.7 32.9 %fusion = bf16[4,2496,768]{2,1,0:T(8,128)(2,1)} fusion(f32[4,768,2496]{1,2,0:T(8,128)} %get-tuple-element.30, bf16[2496,768,1]{1,0,2:T(8,128)(2,1)S(1)} %bitcast.152, bf16[1,768,768]{2,1,0:T(8,128)(2,1)} %bitcast.16, bf16[1,768,768]{2,1,0:T(8,128)(2,1)} %bitcast.14, bf16[1,768,768]{2,1,0:T(8,128)(2,1)} %copy-done.9, bf16[1,768,768]{2,1,0:T(8,128)(2,1)} %bitcast.12), kind=kOutput, calls=%fused_computation.9 | convolution fusion | flops 11899699200 | bytes 54558720 | tf_op jit(solution)/shard_map/rd,kfd->krf/dot_general | solution.py:95
  312.6 16.7 %bitcast_convert_fusion = bf16[2496,768]{1,0:T(8,128)(2,1)S(1)} fusion(bf16[4,2496,768]{2,1,0:T(8,128)(2,1)} %fusion, bf16[1,768,768]{2,1,0:T(8,128)(2,1)} %bitcast.160, bf16[1,768,768]{2,1,0:T(8,128)(2,1)} %bitcast.162, bf16[1,768,768]{2,1,0:T(8,128)(2,1)S(1)} %copy-done.8, bf16[1,768,768]{2,1,0:T(8,128)(2,1)} %bitcast.2), kind=kOutput, calls=%fused_computation.28 | convolution fusion | flops 11786600448 | bytes 23887872 | tf_op jit(solution)/shard_map/krf,kdf->rd/dot_general | solution.py:97
  329.3 49.1 %all_to_all.37 = bf16[8,312,768]{2,1,0:T(8,128)(2,1)} all-to-all(bf16[8,312,768]{2,1,0:T(8,128)(2,1)S(1)} %bitcast.156), channel_id=1, replica_groups=mesh['dp'=1,'tp'=4,'ep'=8] {'ep'}, dimensions={0} | all-to-all | bytes 7667712 | tf_op jit(solution)/shard_map/all_to_all | solution.py:69
  378.7 16.5 %gather_fusion.4 = bf16[2496,768]{1,0:T(8,128)(2,1)} fusion(bf16[8192,768]{1,0:T(8,128)(2,1)} %param.6, s32[3072]{0:T(1024)S(1)} %pad_clamp_fusion), kind=kCustom, calls=%fused_computation.4 | custom fusion | bytes 7677696 | tf_op jit(solution)/shard_map/jit(_take)/gather | solution.py:73
  401.1 16.6 %gather_fusion.5 = bf16[2496,768]{1,0:T(8,128)(2,1)} fusion(bf16[8192,768]{1,0:T(8,128)(2,1)} %param.7, s32[3072]{0:T(1024)S(1)} %pad_clamp_fusion), kind=kCustom, calls=%fused_computation.5 | custom fusion | bytes 7677696 | tf_op jit(solution)/shard_map/jit(_take)/gather | solution.py:74
  421.6 8.6 %fusion.96 = (f32[8192]{0:T(1024)S(1)}, f32[8192,32]{0,1:T(8,128)S(1)}) fusion(bf16[8192,768]{1,0:T(8,128)(2,1)} %param.6, bf16[768,32]{0,1:T(8,128)(2,1)S(1)} %copy-done), kind=kOutput, calls=%fused_computation.187 | convolution fusion | flops 402907136 | bytes 13713408 | tf_op jit(solution)/shard_map/dot_general | solution.py:126
  434.5 8.1 %fusion.17 = f32[768,768]{1,0:T(8,128)} fusion(bf16[2496,768]{1,0:T(8,128)(2,1)} %bitcast.8, bf16[4,2496,768]{2,1,0:T(8,128)(2,1)} %fusion), kind=kOutput, calls=%fused_computation.48 | convolution fusion | flops 2944401408 | bytes 10027008 | tf_op jit(solution)/shard_map/dot_general | solution.py:111
  451.8 8.2 %fusion.16 = f32[768,768]{1,0:T(8,128)} fusion(bf16[2496,768]{1,0:T(8,128)(2,1)} %bitcast.8, bf16[4,2496,768]{2,1,0:T(8,128)(2,1)} %fusion), kind=kOutput, calls=%fused_computation.46 | convolution fusion | flops 2944401408 | bytes 10027008 | tf_op jit(solution)/shard_map/dot_general | solution.py:111
  462.7 6.8 fusion.14
  469.5 6.9 fusion.13
  479.5 8.7 %fusion.23 = f32[2496,768]{1,0:T(8,128)} fusion(bf16[2496,768]{1,0:T(8,128)(2,1)} %bitcast.32, bf16[4,768,768]{2,1,0:T(8,128)(2,1)} %param.9, s32[]{:T(128)S(6)} %select_n.222), kind=kOutput, calls=%fused_computation.60 | convolution fusion | flops 2944401408 | bytes 12681220 | tf_op jit(solution)/shard_map/dot_general | solution.py:105
  492.7 8.0 %bitcast_dynamic-update-slice_fusion.7 = f32[4,768,768]{2,1,0:T(8,128)} fusion(f32[4,768,768]{2,1,0:T(8,128)} %broadcast.181.clone, s32[]{:T(128)S(6)} %select_n.214, bf16[2496,768]{1,0:T(8,128)(2,1)} %bitcast.8, bf16[4,2496,768]{2,1,0:T(8,128)(2,1)} %fusion), kind=kOutput, calls=%fused_computation.59 | convolution fusion | flops 2944401408 | bytes 10027012 | tf_op jit(solution)/shard_map/dot_general | solution.py:111
  512.1 19.2 %bitcast_dynamic-update-slice_fusion.6 = f32[4,768,768]{2,1,0:T(8,128)} fusion(f32[4,768,768]{2,1,0:T(8,128)} %bitcast_dynamic-update-slice_fusion.7, s32[]{:T(128)S(6)} %select_n.222, bf16[2496,768]{1,0:T(8,128)(2,1)} %bitcast.32, f32[2496,768]{1,0:T(8,128)} %fusion.23, bf16[2496,768]{1,0:T(8,128)(2,1)} %bitcast.34, bf16[4,768,768]{2,1,0:T(8,128)(2,1)} %param.10), kind=kOutput, calls=%fused_computation.58 | convolution fusion | flops 5917556736 | bytes 18875392 | tf_op jit(solution)/shard_map/dot_general | solution.py:111
  536.9 7.2 bitcast_dynamic-update-slice_fusion.3
  544.1 7.4 bitcast_dynamic-update-slice_fusion.2
  551.5 13.9 %collective-permute-done.6 = f32[768,768]{1,0:T(8,128)} collective-permute-done((f32[768,768]{1,0:T(8,128)}, f32[768,768]{1,0:T(8,128)}, u32[]{:S(2)}, u32[]{:S(2)}) %collective-permute-start.6) | collective-permute-done | bytes 2359328 | tf_op jit(solution)/shard_map/ppermute | solution.py:116
  568.6 48.0 %collective-permute-done.8 = f32[768,768]{1,0:T(8,128)} collective-permute-done((f32[768,768]{1,0:T(8,128)}, f32[768,768]{1,0:T(8,128)}, u32[]{:S(2)}, u32[]{:S(2)}) %collective-permute-start.8) | collective-permute-done | bytes 2359328 | tf_op jit(solution)/shard_map/ppermute | solution.py:116
  629.7 13.1 %pad_maximum_fusion = bf16[9984,768]{1,0:T(8,128)(2,1)} fusion(bf16[9984,512]{1,0:T(8,128)(2,1)} %all-gather.6.cloned.1.call-done, bf16[9984,256]{1,0:T(8,128)(2,1)} %bitcast.143), kind=kLoop, calls=%fused_computation.19 | loop fusion | flops 30670848 | bytes 30670848 | tf_op jit(solution)/shard_map/concatenate | solution.py:131
  642.8 44.4 %gather_fusion.1 = bf16[8192,768]{1,0:T(8,128)(2,1)} fusion(bf16[9984,768]{1,0:T(8,128)(2,1)} %pad_maximum_fusion, s32[8192]{0:T(1024)S(1)} %copy-done.13), kind=kCustom, calls=%fused_computation.1 | custom fusion | bytes 25198592 | tf_op jit(solution)/shard_map/jit(_take)/gather | solution.py:132
  687.2 16.7 %fusion.4 = (f32[8192]{0:T(1024)S(1)}, bf16[8192,768]{1,0:T(8,128)(2,1)}) fusion(bf16[8192,768]{1,0:T(8,128)(2,1)} %param.7, bf16[8192,768]{1,0:T(8,128)(2,1)} %gather_fusion.1, pred[8192]{0:T(1024)(128)(4,1)S(1)} %copy-done.16, f32[8192]{0:T(1024)S(1)} %copy-done.10), kind=kLoop, calls=%fused_computation.17 | loop fusion | flops 44032000 | bytes 37822464 | tf_op jit(solution)/shard_map/reduce_sum | solution.py:135
  703.8 7.4 convolution_bitcast_fusion
  711.4 44.4 %gather_fusion.3 = bf16[8192,768]{1,0:T(8,128)(2,1)} fusion(bf16[9984,768]{1,0:T(8,128)(2,1)} %all-gather.8.cloned.1.call-done, s32[8192]{0:T(1024)S(1)} %copy-done.13), kind=kCustom, calls=%fused_computation.3 | custom fusion | bytes 25198592 | tf_op jit(solution)/shard_map/jit(_take)/gather | solution.py:133
  755.7 11.1 %add_convert_fusion = bf16[8192,768]{1,0:T(8,128)(2,1)} fusion(bf16[8192,768]{1,0:T(8,128)(2,1)} %gather_fusion.3, pred[8192]{0:T(1024)(128)(4,1)S(1)} %copy-done.16, bf16[768,32]{0,1:T(8,128)(2,1)S(1)} %copy-done, f32[8192]{0:T(1024)S(1)} %copy-done.10, f32[8192]{0:T(1024)S(1)} %get-tuple-element.9, s32[8192]{0:T(1024)S(1)} %copy-done.6, ...), kind=kOutput, calls=%fused_computation.18 | convolution fusion | flops 429916160 | bytes 26435584 | tf_op jit(solution)/shard_map/dot_general | solution.py:137
  (147 shorter events, 112.4 us)
Async XLA Ops:
  7.2 217.7 %copy-start = (bf16[768,32]{0,1:T(8,128)(2,1)S(1)}, bf16[768,32]{0,1:T(8,128)(2,1)}, u32[]{:S(2)}) copy-start(bf16[768,32]{0,1:T(8,128)(2,1)} %param.8) | copy-start | bytes 147460
  33.9 14.6 %slice-start.1 = ((s8[4718592]{0:T(1024)(128)(4,1)}), s8[524288]{0:T(1024)(128)(4,1)S(1)}, s32[]{:S(2)}) async-start(s8[4718592]{0:T(1024)(128)(4,1)} %bitcast.150), calls=%async_computation.12 | async-start | bytes 1048576
  33.9 65.8 %all-to-all-start = ((bf16[8,312,768]{2,1,0:T(8,128)(2,1)}), bf16[8,312,768]{2,1,0:T(8,128)(2,1)}, u32[]{:S(2)}, u32[]{:S(2)}) async-start(bf16[8,312,768]{2,1,0:T(8,128)(2,1)} %bitcast.141), calls=%async_computation | async-start | bytes 7667712 | tf_op jit(solution)/shard_map/all_to_all | solution.py:69
  40.5 460.2 %all-gather.4.cloned.1.call-start = ((), (), s32[]{:S(2)}) async-start(), calls=%async_computation.7 | async-start | bytes 6389760 | tf_op jit(solution)/shard_map/all_gather | solution.py:90
  43.3 56.5 %copy-start.7 = (bf16[1,768,768]{2,1,0:T(8,128)(2,1)}, bf16[1,768,768]{2,1,0:T(8,128)(2,1)S(1)}, u32[]{:S(2)}) copy-start(bf16[1,768,768]{2,1,0:T(8,128)(2,1)S(1)} %get-tuple-element.17) | copy-start | bytes 3538948
  43.3 30.3 %collective-permute-start.2 = (bf16[768,768]{1,0:T(8,128)(2,1)S(1)}, bf16[768,768]{1,0:T(8,128)(2,1)S(1)}, u32[]{:S(2)}, u32[]{:S(2)}) collective-permute-start(bf16[768,768]{1,0:T(8,128)(2,1)S(1)} %get-tuple-element.18), channel_id=1, source_target_pairs={{0,8},{8,16},{16,24},{24,0},{1,9},{9,17},{17,25},{25,1},{2,10},{10... | collective-permute-start | bytes 3538952 | tf_op jit(solution)/shard_map/ppermute | solution.py:32
  44.8 30.2 %collective-permute-start.1 = (bf16[768,768]{1,0:T(8,128)(2,1)S(1)}, bf16[768,768]{1,0:T(8,128)(2,1)S(1)}, u32[]{:S(2)}, u32[]{:S(2)}) collective-permute-start(bf16[768,768]{1,0:T(8,128)(2,1)S(1)} %get-tuple-element.16), channel_id=1, source_target_pairs={{0,24},{8,0},{16,8},{24,16},{1,25},{9,1},{17,9},{25,17},{2,26},{10... | collective-permute-start | bytes 3538952 | tf_op jit(solution)/shard_map/ppermute | solution.py:32
  47.4 52.3 %collective-permute-start = (bf16[768,768]{1,0:T(8,128)(2,1)S(1)}, bf16[768,768]{1,0:T(8,128)(2,1)}, u32[]{:S(2)}, u32[]{:S(2)}) collective-permute-start(bf16[768,768]{1,0:T(8,128)(2,1)S(1)} %get-tuple-element.15), channel_id=1, source_target_pairs={{0,16},{8,24},{16,0},{24,8},{1,17},{9,25},{17,1},{25,9},{2,18},{10... | collective-permute-start | bytes 3538952 | tf_op jit(solution)/shard_map/ppermute | solution.py:32
  50.4 99.9 %copy-start.9 = (bf16[1,768,768]{2,1,0:T(8,128)(2,1)}, bf16[1,768,768]{2,1,0:T(8,128)(2,1)S(1)}, u32[]{:S(2)}) copy-start(bf16[1,768,768]{2,1,0:T(8,128)(2,1)S(1)} %get-tuple-element.13) | copy-start | bytes 3538948
  50.4 75.1 %collective-permute-start.5 = (bf16[768,768]{1,0:T(8,128)(2,1)}, bf16[768,768]{1,0:T(8,128)(2,1)}, u32[]{:S(2)}, u32[]{:S(2)}) collective-permute-start(bf16[768,768]{1,0:T(8,128)(2,1)} %get-tuple-element.14), channel_id=1, source_target_pairs={{0,8},{8,16},{16,24},{24,0},{1,9},{9,17},{17,25},{25,1},{2,10},{10... | collective-permute-start | bytes 3538952 | tf_op jit(solution)/shard_map/ppermute | solution.py:32
  51.3 74.3 %collective-permute-start.4 = (bf16[768,768]{1,0:T(8,128)(2,1)}, bf16[768,768]{1,0:T(8,128)(2,1)}, u32[]{:S(2)}, u32[]{:S(2)}) collective-permute-start(bf16[768,768]{1,0:T(8,128)(2,1)} %get-tuple-element.12), channel_id=1, source_target_pairs={{0,24},{8,0},{16,8},{24,16},{1,25},{9,1},{17,9},{25,17},{2,26},{10... | collective-permute-start | bytes 3538952 | tf_op jit(solution)/shard_map/ppermute | solution.py:32
  73.5 76.8 %collective-permute-start.3 = (bf16[768,768]{1,0:T(8,128)(2,1)}, bf16[768,768]{1,0:T(8,128)(2,1)}, u32[]{:S(2)}, u32[]{:S(2)}) collective-permute-start(bf16[768,768]{1,0:T(8,128)(2,1)} %get-tuple-element.11), channel_id=1, source_target_pairs={{0,16},{8,24},{16,0},{24,8},{1,17},{9,25},{17,1},{25,9},{2,18},{10... | collective-permute-start | bytes 3538952 | tf_op jit(solution)/shard_map/ppermute | solution.py:32
  169.3 460.4 %all-gather.6.cloned.1.call-start = ((), (), s32[]{:S(2)}) async-start(), calls=%async_computation.8 | async-start | bytes 12779520 | tf_op jit(solution)/shard_map/all_gather | solution.py:92
  207.6 503.7 %all-gather.8.cloned.1.call-start = ((), (), s32[]{:S(2)}) async-start(), calls=%async_computation.9 | async-start | bytes 19169280 | tf_op jit(solution)/shard_map/all_gather | solution.py:99
  279.7 32.9 %copy-start.3 = (bf16[8,312,768]{2,1,0:T(8,128)(2,1)}, bf16[8,312,768]{2,1,0:T(8,128)(2,1)S(1)}, u32[]{:S(2)}) copy-start(bf16[8,312,768]{2,1,0:T(8,128)(2,1)S(1)} %all_to_all.36) | copy-start | bytes 11501572
  279.7 32.9 %copy-start.8 = (bf16[1,768,768]{2,1,0:T(8,128)(2,1)S(1)}, bf16[1,768,768]{2,1,0:T(8,128)(2,1)}, u32[]{:S(2)}) copy-start(bf16[1,768,768]{2,1,0:T(8,128)(2,1)} %copy-done.7) | copy-start | bytes 3538948
  329.3 49.2 %copy-start.15 = (f32[24,312]{1,0:T(8,128)S(1)}, f32[24,312]{1,0:T(8,128)}, u32[]{:S(2)}) copy-start(f32[24,312]{1,0:T(8,128)} %copy-done.14) | copy-start | bytes 89860
  329.3 49.2 %copy-start.19 = (s32[8]{0:T(128)S(1)}, s32[8]{0:T(128)}, u32[]{:S(2)}) copy-start(s32[8]{0:T(128)} %get-tuple-element.37) | copy-start | bytes 100
  395.2 50.8 %all-to-all-start.5 = ((bf16[8,312,768]{2,1,0:T(8,128)(2,1)}), bf16[8,312,768]{2,1,0:T(8,128)(2,1)}, u32[]{:S(2)}, u32[]{:S(2)}) async-start(bf16[8,312,768]{2,1,0:T(8,128)(2,1)} %bitcast.142), calls=%async_computation.5 | async-start | bytes 7667712 | tf_op jit(solution)/shard_map/all_to_all | solution.py:69
  401.1 16.6 %copy-start.18 = (s32[8]{0:T(128)S(1)}, s32[8]{0:T(128)}, u32[]{:S(2)}) copy-start(s32[8]{0:T(128)} %copy-done.17) | copy-start | bytes 100
  446.0 59.9 %all-to-all-start.6 = ((bf16[8,312,768]{2,1,0:T(8,128)(2,1)}), bf16[8,312,768]{2,1,0:T(8,128)(2,1)}, u32[]{:S(2)}, u32[]{:S(2)}) async-start(bf16[8,312,768]{2,1,0:T(8,128)(2,1)} %fusion.7), calls=%async_computation.6 | async-start | bytes 7667712 | tf_op jit(solution)/shard_map/all_to_all | solution.py:69
  451.8 10.9 %copy-start.4 = (bf16[8,312,768]{2,1,0:T(8,128)(2,1)S(1)}, bf16[8,312,768]{2,1,0:T(8,128)(2,1)}, u32[]{:S(2)}) copy-start(bf16[8,312,768]{2,1,0:T(8,128)(2,1)} %copy-done.3) | copy-start | bytes 11501572
  460.0 105.3 %collective-permute-start.6 = (f32[768,768]{1,0:T(8,128)}, f32[768,768]{1,0:T(8,128)}, u32[]{:S(2)}, u32[]{:S(2)}) collective-permute-start(f32[768,768]{1,0:T(8,128)} %fusion.17), channel_id=1, source_target_pairs={{0,8},{8,16},{16,24},{24,0},{1,9},{9,17},{17,25},{25,1},{2,10},{10... | collective-permute-start | bytes 7077896 | tf_op jit(solution)/shard_map/ppermute | solution.py:116
  460.6 159.2 %collective-permute-start.7 = (f32[768,768]{1,0:T(8,128)}, f32[768,768]{1,0:T(8,128)S(1)}, u32[]{:S(2)}, u32[]{:S(2)}) collective-permute-start(f32[768,768]{1,0:T(8,128)} %fusion.16), channel_id=1, source_target_pairs={{0,24},{8,0},{16,8},{24,16},{1,25},{9,1},{17,9},{25,17},{2,26},{10... | collective-permute-start | bytes 7077896 | tf_op jit(solution)/shard_map/ppermute | solution.py:117
  469.5 147.0 %collective-permute-start.8 = (f32[768,768]{1,0:T(8,128)}, f32[768,768]{1,0:T(8,128)}, u32[]{:S(2)}, u32[]{:S(2)}) collective-permute-start(f32[768,768]{1,0:T(8,128)} %fusion.14), channel_id=1, source_target_pairs={{0,8},{8,16},{16,24},{24,0},{1,9},{9,17},{17,25},{25,1},{2,10},{10... | collective-permute-start | bytes 7077896 | tf_op jit(solution)/shard_map/ppermute | solution.py:116
  476.4 145.0 %collective-permute-start.9 = (f32[768,768]{1,0:T(8,128)}, f32[768,768]{1,0:T(8,128)}, u32[]{:S(2)}, u32[]{:S(2)}) collective-permute-start(f32[768,768]{1,0:T(8,128)} %fusion.13), channel_id=1, source_target_pairs={{0,24},{8,0},{16,8},{24,16},{1,25},{9,1},{17,9},{25,17},{2,26},{10... | collective-permute-start | bytes 7077896 | tf_op jit(solution)/shard_map/ppermute | solution.py:117
  505.9 118.7 %all-to-all-start.1 = ((bf16[4,8,312,256]{3,2,0,1:T(8,128)(2,1)}), bf16[4,8,312,256]{3,2,0,1:T(8,128)(2,1)}, u32[]{:S(2)}, u32[]{:S(2)}) async-start(bf16[4,8,312,256]{3,2,0,1:T(8,128)(2,1)} %copy.11), calls=%async_computation.1 | async-start | bytes 10223616 | tf_op jit(solution)/shard_map/all_to_all | solution.py:93
  511.9 255.0 %all-reduce.2.cloned.1.call-start = ((), (), s32[]{:S(2)}) async-start(), calls=%async_computation.10 | async-start | bytes 196608 | tf_op jit(solution)/shard_map/psum | solution.py:139
  531.3 12.8 %slice-start.3 = ((s8[7667712]{0:T(1024)(128)(4,1)}), s8[4194304]{0:T(1024)(128)(4,1)S(1)}, s32[]{:S(2)}) async-start(s8[7667712]{0:T(1024)(128)(4,1)} %bitcast.163), calls=%async_computation.14 | async-start | bytes 8388608
  629.7 13.1 %copy-start.13 = (s32[8192]{0:T(1024)S(1)}, s32[8192]{0:T(1024)}, u32[]{:S(2)}) copy-start(s32[8192]{0:T(1024)} %get-tuple-element.27) | copy-start | bytes 98308
  642.7 44.4 %copy-start.10 = (f32[8192]{0:T(1024)S(1)}, f32[8192]{0:T(1024)}, u32[]{:S(2)}) copy-start(f32[8192]{0:T(1024)} %select_reduce_fusion.1) | copy-start | bytes 98308
  642.7 44.4 %copy-start.16 = (pred[8192]{0:T(1024)(128)(4,1)S(1)}, pred[8192]{0:T(1024)(128)(4,1)}, u32[]{:S(2)}) copy-start(pred[8192]{0:T(1024)(128)(4,1)} %broadcast_compare_fusion) | copy-start | bytes 24580
  (13 other events, 60.0 us)
Sparse Core Ops, SparseCore 0:
  169.4 53.8 all-gather.3
  224.9 96.4 all-gather.5
  378.6 189.9 all-gather.7
  711.4 50.0 all-reduce.1

commit v3 on v2

--- a/solution.py
+++ b/solution.py
@@ -1,6 +1,7 @@
 import jax
 import jax.numpy as jnp
 from jax import lax
+from jax.experimental import pallas as pl
 from jax.sharding import PartitionSpec as P
 
 
@@ -85,10 +86,15 @@
 
         pre_act = jnp.einsum("rd,kdf->krf", x_rows, wi, preferred_element_type=f32)
         hidden, slope = gelu_and_slope(pre_act)
-        y_rows = jnp.einsum("krf,kfd->rd", hidden, wo, preferred_element_type=f32).astype(bf16)
         early = d_model // 3
-        y_early = lax.all_gather(y_rows[:, :early], "tp", axis=0, tiled=True).reshape(tp_size, ep_size, cap, early)
-        y_back = exchange(y_rows[:, early:])
+
+        def y_columns(part):
+            return jnp.einsum("krf,kfd->rd", hidden, part, preferred_element_type=f32).astype(bf16)
+
+        y_first = y_columns(wo[:, :, :early])
+        y_rest = y_columns(wo[:, :, early:])
+        y_early = lax.all_gather(y_first, "tp", axis=0, tiled=True).reshape(tp_size, ep_size, cap, early)
+        y_back = exchange(y_rest)
         y_all = lax.all_gather(y_back, "tp", axis=0, tiled=True)
         y_early = lax.all_to_all(y_early, "ep", 1, 1, tiled=True).reshape(-1, early)
 
@@ -115,7 +121,11 @@
             far = rows_product(far_left, far_right)
             up = lax.ppermute(nxt, "tp", [(i, (i + 1) % tp_size) for i in range(tp_size)])
             down = lax.ppermute(prv, "tp", [(i, (i - 1) % tp_size) for i in range(tp_size)])
-            grads = jnp.zeros((local_experts,) + own.shape, f32)
+            grads = pl.pallas_call(
+                lambda ref: None,
+                out_shape=jax.ShapeDtypeStruct((local_experts,) + own.shape, f32),
+                out_specs=pl.BlockSpec(memory_space=pl.ANY),
+            )()
             for part, offset in ((own, 0), (far, 2), (up, 3), (down, 1)):
                 grads = lax.dynamic_update_index_in_dim(grads, part, (my_tp + offset) % tp_size, 0)
             return grads

time: 784 us -> 787 us (level)
  local copies, waits for them, and re-layouts: 202 us -> 187 us
  matrix products: 210 us -> 220 us
    another operation x2 -> x0, local copies, waits for them, and re-layouts: 10.1 us -> none
    dot_general x1 -> x2, matrix products: 15.9 us -> 22.9 us  [y_columns(): jnp.einsum('krf,kfd->rd', hidden, part, preferred_element_type=f32)]
where the time goes in v3:
time: 787 us; the launch traced here: 778 us
  matrix products  220 us (28%)
  local copies, waits for them, and re-layouts  187 us (24%)
  waiting for transfers between devices  141 us (18%)
  blocking collectives  135 us (17%)
  other arithmetic  41 us (5%)
  starting transfers between devices  39.8 us (5%)
  between operations  14.7 us (2%)
    all_to_all x3, blocking collectives, exchange(): lax.all_to_all(rows.reshape(ep_size, cap, rows.shape[1]), 'ep', 0, 0, til...  135 us
    dot_general x8, matrix products, rows_product(): lax.dot_general(left, right, (((0,), (0,)), ((), ())), preferred_element_...  75 us
    ppermute x2, waiting for transfers between devices, spread(): lax.ppermute(nxt, 'tp', [(i, (i + 1) % tp_size) for i in range(tp_size)])  69.1 us
    ppermute x6, waiting for transfers between devices, from_offset(): lax.ppermute(mine, 'tp', [(i, (i - offset) % tp_size) for i in range(tp_s...  69 us
    gather x1, local copies, waits for them, and re-layouts, block(): jnp.take(y_all, slot_row, axis=0, mode='clip')  44.4 us
    gather x1, local copies, waits for them, and re-layouts, block(): jnp.take(s_all, slot_row, axis=0, mode='clip')  44.4 us
    gather x2, local copies, waits for them, and re-layouts, send_rows(): gy_send = jnp.take(grad_out, slot_token, axis=0, mode='clip')  33.1 us
    gather x2, local copies, waits for them, and re-layouts, send_rows(): x_send = jnp.take(tokens, slot_token, axis=0, mode='clip')  33 us
  transfers between devices with their start and end apart: 18, of which 6 were waited for; matrix products, arithmetic and copies ran while one was open for 52% of the time, Pallas kernels for 0%

profile of v3, /device:TPU:97, one launch (start us, length us, event | category | flops | bytes accessed | tf_op | source)
XLA Modules:
  0.0 778.5 jit_solution(8066160476635890344)
XLA Ops:
  17.5 16.5 %gather_fusion = bf16[2496,768]{1,0:T(8,128)(2,1)} fusion(bf16[8192,768]{1,0:T(8,128)(2,1)} %param.6, s32[3072]{0:T(1024)S(1)} %pad_clamp_fusion.1), kind=kCustom, calls=%fused_computation | custom fusion | bytes 7677696 | tf_op jit(solution)/shard_map/jit(_take)/gather | solution.py:74
  53.3 20.2 %collective-permute-done.2 = bf16[768,768]{1,0:T(8,128)(2,1)S(1)} collective-permute-done((bf16[768,768]{1,0:T(8,128)(2,1)S(1)}, bf16[768,768]{1,0:T(8,128)(2,1)S(1)}, u32[]{:S(2)}, u32[]{:S(2)}) %collective-permute-start.2) | collective-permute-done | bytes 1179680 | tf_op jit(solution)/shard_map/ppermute | solution.py:33
  76.0 23.7 %collective-permute-done = bf16[768,768]{1,0:T(8,128)(2,1)} collective-permute-done((bf16[768,768]{1,0:T(8,128)(2,1)S(1)}, bf16[768,768]{1,0:T(8,128)(2,1)}, u32[]{:S(2)}, u32[]{:S(2)}) %collective-permute-start) | collective-permute-done | bytes 1179680 | tf_op jit(solution)/shard_map/ppermute | solution.py:33
  99.8 25.5 %fusion.2 = (bf16[4,2496,768]{2,1,0:T(8,128)(2,1)}, f32[4,768,2496]{1,2,0:T(8,128)}) fusion(bf16[2496,768,1]{1,0,2:T(8,128)(2,1)} %bitcast.9, bf16[1,768,768]{2,1,0:T(8,128)(2,1)} %bitcast.164, bf16[1,768,768]{2,1,0:T(8,128)(2,1)} %bitcast.166, bf16[1,768,768]{2,1,0:T(8,128)(2,1)S(1)} %get-tuple-element.17, bf16[1,768,768]{2,1,0:T(8,128)(2,1)} %bitcast.2), kind=kOutput, calls=%fused_computation.15 | convolution fusion | flops 11857821696 | bytes 54558720 | tf_op jit(solution)/shard_map/rd,kdf->krf/dot_general | solution.py:87
  125.2 25.1 %collective-permute-done.3 = bf16[768,768]{1,0:T(8,128)(2,1)} collective-permute-done((bf16[768,768]{1,0:T(8,128)(2,1)}, bf16[768,768]{1,0:T(8,128)(2,1)}, u32[]{:S(2)}, u32[]{:S(2)}) %collective-permute-start.3) | collective-permute-done | bytes 1179680 | tf_op jit(solution)/shard_map/ppermute | solution.py:33
  150.3 10.8 %fusion.20 = bf16[2496,256]{1,0:T(8,128)(2,1)} fusion(bf16[4,2496,768]{2,1,0:T(8,128)(2,1)} %get-tuple-element.29, bf16[1,768,768]{2,1,0:T(8,128)(2,1)} %bitcast.16, bf16[1,768,768]{2,1,0:T(8,128)(2,1)} %bitcast.14, bf16[1,768,768]{2,1,0:T(8,128)(2,1)S(1)} %get-tuple-element.13, bf16[1,768,768]{2,1,0:T(8,128)(2,1)} %bitcast.12), kind=kOutput, calls=%fused_computation.46 | convolution fusion | flops 3932798976 | bytes 21331968 | tf_op jit(solution)/shard_map/krf,kfd->rd/dot_general | solution.py:92
  161.3 12.1 %bitcast_convert_fusion.1 = bf16[2496,512]{1,0:T(8,128)(2,1)S(1)} fusion(bf16[4,2496,768]{2,1,0:T(8,128)(2,1)} %get-tuple-element.29, bf16[1,768,768]{2,1,0:T(8,128)(2,1)} %bitcast.16, bf16[1,768,768]{2,1,0:T(8,128)(2,1)} %bitcast.14, bf16[1,768,768]{2,1,0:T(8,128)(2,1)S(1)} %get-tuple-element.13, bf16[1,768,768]{2,1,0:T(8,128)(2,1)} %bitcast.12), kind=kOutput, calls=%fused_computation.34 | convolution fusion | flops 7865597952 | bytes 22609920 | tf_op jit(solution)/shard_map/krf,kfd->rd/dot_general | solution.py:92
  173.4 37.0 %all_to_all.35 = bf16[8,312,512]{2,1,0:T(8,128)(2,1)} all-to-all(bf16[8,312,512]{2,1,0:T(8,128)(2,1)S(1)} %bitcast.161), channel_id=1, replica_groups=mesh['dp'=1,'tp'=4,'ep'=8] {'ep'}, dimensions={0} | all-to-all | bytes 5111808 | tf_op jit(solution)/shard_map/all_to_all | solution.py:70
  210.6 16.5 %gather_fusion.2 = bf16[2496,768]{1,0:T(8,128)(2,1)} fusion(bf16[8192,768]{1,0:T(8,128)(2,1)} %param.7, s32[3072]{0:T(1024)S(1)} %pad_clamp_fusion.1), kind=kCustom, calls=%fused_computation.2 | custom fusion | bytes 7677696 | tf_op jit(solution)/shard_map/jit(_take)/gather | solution.py:75
  234.1 48.5 %all_to_all.36 = bf16[8,312,768]{2,1,0:T(8,128)(2,1)S(1)} all-to-all(bf16[8,312,768]{2,1,0:T(8,128)(2,1)S(1)} %fusion.8), channel_id=1, replica_groups=mesh['dp'=1,'tp'=4,'ep'=8] {'ep'}, dimensions={0} | all-to-all | bytes 7667712 | tf_op jit(solution)/shard_map/all_to_all | solution.py:70
  282.7 32.9 %fusion = bf16[4,2496,768]{2,1,0:T(8,128)(2,1)} fusion(f32[4,768,2496]{1,2,0:T(8,128)} %get-tuple-element.30, bf16[2496,768,1]{1,0,2:T(8,128)(2,1)S(1)} %bitcast.156, bf16[1,768,768]{2,1,0:T(8,128)(2,1)} %bitcast.16, bf16[1,768,768]{2,1,0:T(8,128)(2,1)} %bitcast.14, bf16[1,768,768]{2,1,0:T(8,128)(2,1)} %copy-done.5, bf16[1,768,768]{2,1,0:T(8,128)(2,1)} %bitcast.12), kind=kOutput, calls=%fused_computation.9 | convolution fusion | flops 11899699200 | bytes 54558720 | tf_op jit(solution)/shard_map/rd,kfd->krf/dot_general | solution.py:101
  315.5 16.7 %bitcast_convert_fusion = bf16[2496,768]{1,0:T(8,128)(2,1)S(1)} fusion(bf16[4,2496,768]{2,1,0:T(8,128)(2,1)} %fusion, bf16[1,768,768]{2,1,0:T(8,128)(2,1)} %bitcast.165, bf16[1,768,768]{2,1,0:T(8,128)(2,1)} %bitcast.167, bf16[1,768,768]{2,1,0:T(8,128)(2,1)S(1)} %get-tuple-element.17, bf16[1,768,768]{2,1,0:T(8,128)(2,1)} %bitcast.2), kind=kOutput, calls=%fused_computation.28 | convolution fusion | flops 11786600448 | bytes 23887872 | tf_op jit(solution)/shard_map/krf,kdf->rd/dot_general | solution.py:103
  332.3 49.1 %all_to_all.37 = bf16[8,312,768]{2,1,0:T(8,128)(2,1)} all-to-all(bf16[8,312,768]{2,1,0:T(8,128)(2,1)S(1)} %bitcast.160), channel_id=1, replica_groups=mesh['dp'=1,'tp'=4,'ep'=8] {'ep'}, dimensions={0} | all-to-all | bytes 7667712 | tf_op jit(solution)/shard_map/all_to_all | solution.py:70
  381.6 16.5 %gather_fusion.4 = bf16[2496,768]{1,0:T(8,128)(2,1)} fusion(bf16[8192,768]{1,0:T(8,128)(2,1)} %param.6, s32[3072]{0:T(1024)S(1)} %pad_clamp_fusion), kind=kCustom, calls=%fused_computation.4 | custom fusion | bytes 7677696 | tf_op jit(solution)/shard_map/jit(_take)/gather | solution.py:74
  403.9 16.6 %gather_fusion.5 = bf16[2496,768]{1,0:T(8,128)(2,1)} fusion(bf16[8192,768]{1,0:T(8,128)(2,1)} %param.7, s32[3072]{0:T(1024)S(1)} %pad_clamp_fusion), kind=kCustom, calls=%fused_computation.5 | custom fusion | bytes 7677696 | tf_op jit(solution)/shard_map/jit(_take)/gather | solution.py:75
  425.0 8.6 %fusion.119 = (f32[8192]{0:T(1024)S(1)}, f32[8192,32]{0,1:T(8,128)S(1)}) fusion(bf16[8192,768]{1,0:T(8,128)(2,1)} %param.6, bf16[768,32]{0,1:T(8,128)(2,1)S(1)} %copy-done), kind=kOutput, calls=%fused_computation.210 | convolution fusion | flops 402907136 | bytes 13713408 | tf_op jit(solution)/shard_map/dot_general | solution.py:136
  438.0 8.1 %fusion.25 = f32[768,768]{1,0:T(8,128)} fusion(bf16[2496,768]{1,0:T(8,128)(2,1)} %bitcast.8, bf16[4,2496,768]{2,1,0:T(8,128)(2,1)} %fusion), kind=kOutput, calls=%fused_computation.56 | convolution fusion | flops 2944401408 | bytes 10027008 | tf_op jit(solution)/shard_map/dot_general | solution.py:117
  454.6 8.2 %fusion.24 = f32[768,768]{1,0:T(8,128)} fusion(bf16[2496,768]{1,0:T(8,128)(2,1)} %bitcast.8, bf16[4,2496,768]{2,1,0:T(8,128)(2,1)} %fusion), kind=kOutput, calls=%fused_computation.54 | convolution fusion | flops 2944401408 | bytes 10027008 | tf_op jit(solution)/shard_map/dot_general | solution.py:117
  472.2 6.8 fusion.21
  482.2 8.7 %fusion.45 = f32[2496,768]{1,0:T(8,128)} fusion(bf16[2496,768]{1,0:T(8,128)(2,1)} %bitcast.33, bf16[4,768,768]{2,1,0:T(8,128)(2,1)} %param.9, s32[]{:T(128)S(6)} %select_n.222), kind=kOutput, calls=%fused_computation.82 | convolution fusion | flops 2944401408 | bytes 12681220 | tf_op jit(solution)/shard_map/dot_general | solution.py:111
  490.9 8.1 %bitcast_dynamic-update-slice_fusion.7 = f32[4,768,768]{2,1,0:T(8,128)} fusion(f32[4,768,768]{2,1,0:T(8,128)} %shard_map.101, s32[]{:T(128)S(6)} %select_n.214, bf16[2496,768]{1,0:T(8,128)(2,1)} %bitcast.8, bf16[4,2496,768]{2,1,0:T(8,128)(2,1)} %fusion), kind=kOutput, calls=%fused_computation.74 | convolution fusion | flops 2944401408 | bytes 10027012 | tf_op jit(solution)/shard_map/dot_general | solution.py:117
  510.3 19.2 %bitcast_dynamic-update-slice_fusion.6 = f32[4,768,768]{2,1,0:T(8,128)} fusion(f32[4,768,768]{2,1,0:T(8,128)} %bitcast_dynamic-update-slice_fusion.7, s32[]{:T(128)S(6)} %select_n.222, bf16[2496,768]{1,0:T(8,128)(2,1)} %bitcast.33, f32[2496,768]{1,0:T(8,128)} %fusion.45, bf16[2496,768]{1,0:T(8,128)(2,1)} %bitcast.35, bf16[4,768,768]{2,1,0:T(8,128)(2,1)} %param.10), kind=kOutput, calls=%fused_computation.73 | convolution fusion | flops 5917556736 | bytes 18875392 | tf_op jit(solution)/shard_map/dot_general | solution.py:117
  529.6 8.2 %bitcast_dynamic-update-slice_fusion.3 = f32[4,768,768]{2,1,0:T(8,128)} fusion(f32[4,768,768]{2,1,0:T(8,128)} %shard_map.102, s32[]{:T(128)S(6)} %select_n.214, bf16[2496,768]{1,0:T(8,128)(2,1)} %bitcast.157, bf16[4,2496,768]{2,1,0:T(8,128)(2,1)} %get-tuple-element.29), kind=kOutput, calls=%fused_computation.70 | convolution fusion | flops 2944401408 | bytes 10027012 | tf_op jit(solution)/shard_map/dot_general | solution.py:117
  537.7 9.6 %bitcast_dynamic-update-slice_fusion.2 = f32[4,768,768]{2,1,0:T(8,128)} fusion(f32[4,768,768]{2,1,0:T(8,128)} %bitcast_dynamic-update-slice_fusion.3, s32[]{:T(128)S(6)} %select_n.222, bf16[2496,768]{1,0:T(8,128)(2,1)} %bitcast.35, f32[2496,768]{1,0:T(8,128)} %fusion.45), kind=kOutput, calls=%fused_computation.69 | convolution fusion | flops 2959736832 | bytes 13860868 | tf_op jit(solution)/shard_map/dot_general | solution.py:117
  547.3 20.8 %collective-permute-done.6 = f32[768,768]{1,0:T(8,128)} collective-permute-done((f32[768,768]{1,0:T(8,128)}, f32[768,768]{1,0:T(8,128)}, u32[]{:S(2)}, u32[]{:S(2)}) %collective-permute-start.6) | collective-permute-done | bytes 2359328 | tf_op jit(solution)/shard_map/ppermute | solution.py:122
  571.3 48.3 %collective-permute-done.8 = f32[768,768]{1,0:T(8,128)} collective-permute-done((f32[768,768]{1,0:T(8,128)}, f32[768,768]{1,0:T(8,128)}, u32[]{:S(2)}, u32[]{:S(2)}) %collective-permute-start.8) | collective-permute-done | bytes 2359328 | tf_op jit(solution)/shard_map/ppermute | solution.py:122
  632.8 13.1 %pad_maximum_fusion = bf16[9984,768]{1,0:T(8,128)(2,1)} fusion(bf16[9984,512]{1,0:T(8,128)(2,1)} %all-gather.6.cloned.1.call-done, bf16[9984,256]{1,0:T(8,128)(2,1)} %bitcast.148), kind=kLoop, calls=%fused_computation.19 | loop fusion | flops 30670848 | bytes 30670848 | tf_op jit(solution)/shard_map/concatenate | solution.py:141
  645.9 44.4 %gather_fusion.1 = bf16[8192,768]{1,0:T(8,128)(2,1)} fusion(bf16[9984,768]{1,0:T(8,128)(2,1)} %pad_maximum_fusion, s32[8192]{0:T(1024)S(1)} %copy-done.9), kind=kCustom, calls=%fused_computation.1 | custom fusion | bytes 25198592 | tf_op jit(solution)/shard_map/jit(_take)/gather | solution.py:142
  690.3 16.7 %fusion.4 = (f32[8192]{0:T(1024)S(1)}, bf16[8192,768]{1,0:T(8,128)(2,1)}) fusion(bf16[8192,768]{1,0:T(8,128)(2,1)} %param.7, bf16[8192,768]{1,0:T(8,128)(2,1)} %gather_fusion.1, pred[8192]{0:T(1024)(128)(4,1)S(1)} %copy-done.12, f32[8192]{0:T(1024)S(1)} %copy-done.6), kind=kLoop, calls=%fused_computation.17 | loop fusion | flops 44032000 | bytes 37822464 | tf_op jit(solution)/shard_map/reduce_sum | solution.py:145
  706.9 7.4 convolution_bitcast_fusion.1
  714.5 44.4 %gather_fusion.3 = bf16[8192,768]{1,0:T(8,128)(2,1)} fusion(bf16[9984,768]{1,0:T(8,128)(2,1)} %all-gather.8.cloned.1.call-done, s32[8192]{0:T(1024)S(1)} %copy-done.9), kind=kCustom, calls=%fused_computation.3 | custom fusion | bytes 25198592 | tf_op jit(solution)/shard_map/jit(_take)/gather | solution.py:143
  758.8 11.1 %add_convert_fusion = bf16[8192,768]{1,0:T(8,128)(2,1)} fusion(bf16[8192,768]{1,0:T(8,128)(2,1)} %gather_fusion.3, pred[8192]{0:T(1024)(128)(4,1)S(1)} %copy-done.12, bf16[768,32]{0,1:T(8,128)(2,1)S(1)} %copy-done, f32[8192]{0:T(1024)S(1)} %copy-done.6, f32[8192]{0:T(1024)S(1)} %get-tuple-element.9, s32[8192]{0:T(1024)S(1)} %copy-done.4, ...), kind=kOutput, calls=%fused_computation.18 | convolution fusion | flops 429916160 | bytes 26435584 | tf_op jit(solution)/shard_map/dot_general | solution.py:147
  (132 shorter events, 104.3 us)
Async XLA Ops:
  7.2 220.0 %copy-start = (bf16[768,32]{0,1:T(8,128)(2,1)S(1)}, bf16[768,32]{0,1:T(8,128)(2,1)}, u32[]{:S(2)}) copy-start(bf16[768,32]{0,1:T(8,128)(2,1)} %param.8) | copy-start | bytes 147460
  33.9 14.6 %slice-start = ((s8[4718592]{0:T(1024)(128)(4,1)}), s8[524288]{0:T(1024)(128)(4,1)S(1)}, s32[]{:S(2)}) async-start(s8[4718592]{0:T(1024)(128)(4,1)} %bitcast.154), calls=%async_computation.11 | async-start | bytes 1048576
  33.9 65.8 %all-to-all-start = ((bf16[8,312,768]{2,1,0:T(8,128)(2,1)}), bf16[8,312,768]{2,1,0:T(8,128)(2,1)}, u32[]{:S(2)}, u32[]{:S(2)}) async-start(bf16[8,312,768]{2,1,0:T(8,128)(2,1)} %bitcast.146), calls=%async_computation | async-start | bytes 7667712 | tf_op jit(solution)/shard_map/all_to_all | solution.py:70
  40.5 458.5 %all-gather.4.cloned.1.call-start = ((), (), s32[]{:S(2)}) async-start(), calls=%async_computation.7 | async-start | bytes 6389760 | tf_op jit(solution)/shard_map/all_gather | solution.py:96
  40.5 8.0 %slice-start.1 = ((s8[4718592]{0:T(1024)(128)(4,1)}), s8[4194304]{0:T(1024)(128)(4,1)S(1)}, s32[]{:S(2)}) async-start(s8[4718592]{0:T(1024)(128)(4,1)} %bitcast.154), calls=%async_computation.12 | async-start | bytes 8388608
  43.3 30.3 %collective-permute-start.2 = (bf16[768,768]{1,0:T(8,128)(2,1)S(1)}, bf16[768,768]{1,0:T(8,128)(2,1)S(1)}, u32[]{:S(2)}, u32[]{:S(2)}) collective-permute-start(bf16[768,768]{1,0:T(8,128)(2,1)S(1)} %get-tuple-element.18), channel_id=1, source_target_pairs={{0,8},{8,16},{16,24},{24,0},{1,9},{9,17},{17,25},{25,1},{2,10},{10... | collective-permute-start | bytes 3538952 | tf_op jit(solution)/shard_map/ppermute | solution.py:33
  44.8 30.2 %collective-permute-start.1 = (bf16[768,768]{1,0:T(8,128)(2,1)S(1)}, bf16[768,768]{1,0:T(8,128)(2,1)S(1)}, u32[]{:S(2)}, u32[]{:S(2)}) collective-permute-start(bf16[768,768]{1,0:T(8,128)(2,1)S(1)} %get-tuple-element.16), channel_id=1, source_target_pairs={{0,24},{8,0},{16,8},{24,16},{1,25},{9,1},{17,9},{25,17},{2,26},{10... | collective-permute-start | bytes 3538952 | tf_op jit(solution)/shard_map/ppermute | solution.py:33
  47.5 52.3 %collective-permute-start = (bf16[768,768]{1,0:T(8,128)(2,1)S(1)}, bf16[768,768]{1,0:T(8,128)(2,1)}, u32[]{:S(2)}, u32[]{:S(2)}) collective-permute-start(bf16[768,768]{1,0:T(8,128)(2,1)S(1)} %get-tuple-element.15), channel_id=1, source_target_pairs={{0,16},{8,24},{16,0},{24,8},{1,17},{9,25},{17,1},{25,9},{2,18},{10... | collective-permute-start | bytes 3538952 | tf_op jit(solution)/shard_map/ppermute | solution.py:33
  50.4 110.8 %copy-start.5 = (bf16[1,768,768]{2,1,0:T(8,128)(2,1)}, bf16[1,768,768]{2,1,0:T(8,128)(2,1)S(1)}, u32[]{:S(2)}) copy-start(bf16[1,768,768]{2,1,0:T(8,128)(2,1)S(1)} %get-tuple-element.13) | copy-start | bytes 3538948
  50.4 74.8 %collective-permute-start.5 = (bf16[768,768]{1,0:T(8,128)(2,1)}, bf16[768,768]{1,0:T(8,128)(2,1)}, u32[]{:S(2)}, u32[]{:S(2)}) collective-permute-start(bf16[768,768]{1,0:T(8,128)(2,1)} %get-tuple-element.14), channel_id=1, source_target_pairs={{0,8},{8,16},{16,24},{24,0},{1,9},{9,17},{17,25},{25,1},{2,10},{10... | collective-permute-start | bytes 3538952 | tf_op jit(solution)/shard_map/ppermute | solution.py:33
  51.3 73.9 %collective-permute-start.4 = (bf16[768,768]{1,0:T(8,128)(2,1)}, bf16[768,768]{1,0:T(8,128)(2,1)}, u32[]{:S(2)}, u32[]{:S(2)}) collective-permute-start(bf16[768,768]{1,0:T(8,128)(2,1)} %get-tuple-element.12), channel_id=1, source_target_pairs={{0,24},{8,0},{16,8},{24,16},{1,25},{9,1},{17,9},{25,17},{2,26},{10... | collective-permute-start | bytes 3538952 | tf_op jit(solution)/shard_map/ppermute | solution.py:33
  73.5 76.8 %collective-permute-start.3 = (bf16[768,768]{1,0:T(8,128)(2,1)}, bf16[768,768]{1,0:T(8,128)(2,1)}, u32[]{:S(2)}, u32[]{:S(2)}) collective-permute-start(bf16[768,768]{1,0:T(8,128)(2,1)} %get-tuple-element.11), channel_id=1, source_target_pairs={{0,16},{8,24},{16,0},{24,8},{1,17},{9,25},{17,1},{25,9},{2,18},{10... | collective-permute-start | bytes 3538952 | tf_op jit(solution)/shard_map/ppermute | solution.py:33
  161.2 471.6 %all-gather.6.cloned.1.call-start = ((), (), s32[]{:S(2)}) async-start(), calls=%async_computation.8 | async-start | bytes 12779520 | tf_op jit(solution)/shard_map/all_gather | solution.py:98
  210.5 504.0 %all-gather.8.cloned.1.call-start = ((), (), s32[]{:S(2)}) async-start(), calls=%async_computation.9 | async-start | bytes 19169280 | tf_op jit(solution)/shard_map/all_gather | solution.py:105
  282.7 32.9 %copy-start.2 = (bf16[8,312,768]{2,1,0:T(8,128)(2,1)}, bf16[8,312,768]{2,1,0:T(8,128)(2,1)S(1)}, u32[]{:S(2)}) copy-start(bf16[8,312,768]{2,1,0:T(8,128)(2,1)S(1)} %all_to_all.36) | copy-start | bytes 11501572
  332.2 49.1 %copy-start.11 = (f32[24,312]{1,0:T(8,128)S(1)}, f32[24,312]{1,0:T(8,128)}, u32[]{:S(2)}) copy-start(f32[24,312]{1,0:T(8,128)} %copy-done.10) | copy-start | bytes 89860
  332.3 49.1 %copy-start.15 = (s32[8]{0:T(128)S(1)}, s32[8]{0:T(128)}, u32[]{:S(2)}) copy-start(s32[8]{0:T(128)} %get-tuple-element.37) | copy-start | bytes 100
  398.1 50.7 %all-to-all-start.5 = ((bf16[8,312,768]{2,1,0:T(8,128)(2,1)}), bf16[8,312,768]{2,1,0:T(8,128)(2,1)}, u32[]{:S(2)}, u32[]{:S(2)}) async-start(bf16[8,312,768]{2,1,0:T(8,128)(2,1)} %bitcast.147), calls=%async_computation.5 | async-start | bytes 7667712 | tf_op jit(solution)/shard_map/all_to_all | solution.py:70
  425.0 8.9 %copy-start.8 = (s32[4,2,8,128]{3,1,2,0:T(2,128)S(1)}, s32[4,2,8,128]{3,1,2,0:T(2,128)}, u32[]{:S(2)}) copy-start(s32[4,2,8,128]{3,1,2,0:T(2,128)} %copy-done.7) | copy-start | bytes 98308
  425.0 9.5 %copy-start.4 = (s32[8192]{0:T(1024)S(1)}, s32[8192]{0:T(1024)}, u32[]{:S(2)}) copy-start(s32[8192]{0:T(1024)} %param.11) | copy-start | bytes 98308
  425.0 10.4 %copy-start.1 = (bf16[2496,768]{1,0:T(8,128)(2,1)S(1)}, bf16[2496,768]{1,0:T(8,128)(2,1)}, u32[]{:S(2)}) copy-start(bf16[2496,768]{1,0:T(8,128)(2,1)} %gather_fusion.5) | copy-start | bytes 11501572
  448.8 55.4 %all-to-all-start.6 = ((bf16[8,312,768]{2,1,0:T(8,128)(2,1)}), bf16[8,312,768]{2,1,0:T(8,128)(2,1)}, u32[]{:S(2)}, u32[]{:S(2)}) async-start(bf16[8,312,768]{2,1,0:T(8,128)(2,1)} %fusion.7), calls=%async_computation.6 | async-start | bytes 7667712 | tf_op jit(solution)/shard_map/all_to_all | solution.py:70
  454.5 10.9 %copy-start.3 = (bf16[8,312,768]{2,1,0:T(8,128)(2,1)S(1)}, bf16[8,312,768]{2,1,0:T(8,128)(2,1)}, u32[]{:S(2)}) copy-start(bf16[8,312,768]{2,1,0:T(8,128)(2,1)} %copy-done.2) | copy-start | bytes 11501572
  462.8 105.3 %collective-permute-start.6 = (f32[768,768]{1,0:T(8,128)}, f32[768,768]{1,0:T(8,128)}, u32[]{:S(2)}, u32[]{:S(2)}) collective-permute-start(f32[768,768]{1,0:T(8,128)} %fusion.25), channel_id=1, source_target_pairs={{0,8},{8,16},{16,24},{24,0},{1,9},{9,17},{17,25},{25,1},{2,10},{10... | collective-permute-start | bytes 7077896 | tf_op jit(solution)/shard_map/ppermute | solution.py:122
  463.6 159.2 %collective-permute-start.7 = (f32[768,768]{1,0:T(8,128)}, f32[768,768]{1,0:T(8,128)S(1)}, u32[]{:S(2)}, u32[]{:S(2)}) collective-permute-start(f32[768,768]{1,0:T(8,128)} %fusion.24), channel_id=1, source_target_pairs={{0,24},{8,0},{16,8},{24,16},{1,25},{9,1},{17,9},{25,17},{2,26},{10... | collective-permute-start | bytes 7077896 | tf_op jit(solution)/shard_map/ppermute | solution.py:123
  472.2 147.4 %collective-permute-start.8 = (f32[768,768]{1,0:T(8,128)}, f32[768,768]{1,0:T(8,128)}, u32[]{:S(2)}, u32[]{:S(2)}) collective-permute-start(f32[768,768]{1,0:T(8,128)} %fusion.22), channel_id=1, source_target_pairs={{0,8},{8,16},{16,24},{24,0},{1,9},{9,17},{17,25},{25,1},{2,10},{10... | collective-permute-start | bytes 7077896 | tf_op jit(solution)/shard_map/ppermute | solution.py:122
  479.1 145.3 %collective-permute-start.9 = (f32[768,768]{1,0:T(8,128)}, f32[768,768]{1,0:T(8,128)}, u32[]{:S(2)}, u32[]{:S(2)}) collective-permute-start(f32[768,768]{1,0:T(8,128)} %fusion.21), channel_id=1, source_target_pairs={{0,24},{8,0},{16,8},{24,16},{1,25},{9,1},{17,9},{25,17},{2,26},{10... | collective-permute-start | bytes 7077896 | tf_op jit(solution)/shard_map/ppermute | solution.py:123
  504.2 123.5 %all-to-all-start.1 = ((bf16[4,8,312,256]{3,2,0,1:T(8,128)(2,1)}), bf16[4,8,312,256]{3,2,0,1:T(8,128)(2,1)}, u32[]{:S(2)}, u32[]{:S(2)}) async-start(bf16[4,8,312,256]{3,2,0,1:T(8,128)(2,1)} %copy.11), calls=%async_computation.1 | async-start | bytes 10223616 | tf_op jit(solution)/shard_map/all_to_all | solution.py:99
  510.2 259.8 %all-reduce.2.cloned.1.call-start = ((), (), s32[]{:S(2)}) async-start(), calls=%async_computation.10 | async-start | bytes 196608 | tf_op jit(solution)/shard_map/psum | solution.py:149
  632.8 13.1 %copy-start.9 = (s32[8192]{0:T(1024)S(1)}, s32[8192]{0:T(1024)}, u32[]{:S(2)}) copy-start(s32[8192]{0:T(1024)} %get-tuple-element.27) | copy-start | bytes 98308
  645.9 44.4 %copy-start.6 = (f32[8192]{0:T(1024)S(1)}, f32[8192]{0:T(1024)}, u32[]{:S(2)}) copy-start(f32[8192]{0:T(1024)} %select_reduce_fusion.1) | copy-start | bytes 98308
  645.9 44.4 %copy-start.12 = (pred[8192]{0:T(1024)(128)(4,1)S(1)}, pred[8192]{0:T(1024)(128)(4,1)}, u32[]{:S(2)}) copy-start(pred[8192]{0:T(1024)(128)(4,1)} %broadcast_compare_fusion) | copy-start | bytes 24580
  (6 other events, 7.4 us)
Sparse Core Ops, SparseCore 0:
  161.3 53.8 all-gather.3
  216.7 96.4 all-gather.5
  381.5 190.2 all-gather.7
  714.5 50.0 all-reduce.1
